TPU v7x, 8 devices: a whole 2x2x1 slice. The times are simulated.
8 devices in a mesh: rows: 2 (over z, y), terms: 4 (over x, core).
Axes of the slice: x: 2, y: 2, z: 1, core: 2. Of those that a mesh axis runs over, the one named last changes fastest.
Arguments:
- wavefunc: float32 [256, 4, 4, 256], replicated
- left_env: bfloat16 [64, 256, 256], P('terms')
- two_site: bfloat16 [64, 16, 16], P('terms')
- right_env: bfloat16 [64, 256, 256], P('terms', 'rows')
Outputs:
- output 1: float32 [7, 256, 4, 4, 256], P(None, 'terms', None, None, 'rows')
- output 2: float32 [6], replicated
- output 3: float32 [6], replicated
All inputs are finite; a program needn't handle non-finite values.
Results may differ from a plain program's by a relative error of at most 0.0120408.
Values are sent between devices in bfloat16 or wider.
A program may use at most 1 GiB of HBM per device.

v0:
```python
import jax
import jax.numpy as jnp
from jax import lax
from jax.sharding import PartitionSpec as P

KRYLOV_STEPS = 6


def local_sigma(full_u, left_loc, two_loc, right_loc):
    right_part = jnp.einsum('cpe,kbe->kcpb', full_u, right_loc, preferred_element_type=jnp.float32).astype(jnp.bfloat16)
    mid_part = jnp.einsum('kqp,kcpb->kcqb', two_loc, right_part, preferred_element_type=jnp.float32).astype(jnp.bfloat16)
    return jnp.einsum('kac,kcqb->aqb', left_loc, mid_part, preferred_element_type=jnp.float32)


def solution(mesh):
    terms_count = mesh.shape['terms']
    rows_count = mesh.shape['rows']

    def body_fn(wavefunc, left_loc, two_loc, right_loc):
        bond_dim = wavefunc.shape[0]
        phys_dim = wavefunc.shape[1]
        pair_dim = phys_dim * phys_dim
        elem_count = float(bond_dim * bond_dim * pair_dim)
        row_block = bond_dim // terms_count
        col_block = bond_dim // rows_count
        term_idx = lax.axis_index('terms')
        row_idx = lax.axis_index('rows')
        init_scale = jnp.sqrt(jnp.mean(wavefunc * wavefunc))
        first_vec = (wavefunc / init_scale).reshape(bond_dim, pair_dim, bond_dim)
        cur_vec = lax.dynamic_slice(first_vec, (term_idx * row_block, 0, row_idx * col_block), (row_block, pair_dim, col_block))
        prev_vec = jnp.zeros_like(cur_vec)
        prev_beta = jnp.zeros((), jnp.float32)
        full_u = first_vec.astype(jnp.bfloat16)
        vec_list = [cur_vec]
        alpha_list = []
        beta_list = []
        for step_idx in range(KRYLOV_STEPS):
            part_sigma = local_sigma(full_u, left_loc, two_loc, right_loc)
            w_vec = lax.psum_scatter(part_sigma, 'terms', scatter_dimension=0, tiled=True)
            alpha_val = lax.psum(jnp.sum(w_vec * cur_vec), ('rows', 'terms')) / elem_count
            w_vec = w_vec - alpha_val * cur_vec - prev_beta * prev_vec
            beta_val = jnp.sqrt(lax.psum(jnp.sum(w_vec * w_vec), ('rows', 'terms')) / elem_count)
            next_vec = w_vec / beta_val
            vec_list.append(next_vec)
            alpha_list.append(alpha_val)
            beta_list.append(beta_val)
            prev_vec, cur_vec, prev_beta = cur_vec, next_vec, beta_val
            if step_idx + 1 < KRYLOV_STEPS:
                col_gather = lax.all_gather(next_vec.astype(jnp.bfloat16), 'rows', axis=2, tiled=True)
                full_u = lax.all_gather(col_gather, 'terms', axis=0, tiled=True)
        krylov = jnp.stack(vec_list).reshape(KRYLOV_STEPS + 1, row_block, phys_dim, phys_dim, col_block)
        return krylov, jnp.stack(alpha_list), jnp.stack(beta_list)

    return jax.shard_map(body_fn, mesh=mesh, in_specs=(P(), P('terms'), P('terms'), P('terms', 'rows')), out_specs=(P(None, 'terms', None, None, 'rows'), P(), P()), check_vma=False)
```

profile of v0, /device:TPU:0, one launch (start us, length us, event | category | flops | bytes accessed | tf_op | source)
XLA Modules:
  0.0 967.0 jit_solution(3694400488699353612)
XLA Ops:
  7.2 5.1 multiply_reduce_fusion
  20.2 8.6 convert_bitcast_fusion.11
  28.8 19.8 %convert_bitcast_fusion.10 = bf16[16,256,16,128]{3,2,1,0:T(8,128)(2,1)} fusion(bf16[16,256,16,128]{3,1,0,2:T(8,128)(2,1)} %convert_bitcast_fusion.11, bf16[16,16,16]{2,1,0:T(8,128)(2,1)S(1)} %copy-done.8), kind=kOutput, calls=%fused_computation.34 | convolution fusion | flops 276824064 | bytes 33562624 | tf_op jit(solution)/shard_map/kqp,kcpb->kcqb/dot_general | solution.py:11
  48.6 15.7 %fusion.49 = f32[256,16,128]{0,2,1:T(8,128)} fusion(bf16[16,256,256]{2,1,0:T(8,128)(2,1)S(1)} %copy-done, bf16[16,256,16,128]{3,2,1,0:T(8,128)(2,1)} %convert_bitcast_fusion.10), kind=kOutput, calls=%fused_computation.51 | convolution fusion | flops 4294967296 | bytes 20971520 | tf_op jit(solution)/shard_map/kac,kcqb->aqb/dot_general | solution.py:12
  67.5 28.5 %reduce-scatter.7.cloned.1.call-done = f32[64,16,128]{2,1,0:T(8,128)} async-done(((f32[256,16,128]{2,1,0:T(8,128)}), f32[64,16,128]{2,1,0:T(8,128)}) %reduce-scatter.7.cloned.1.call-update) | async-done | bytes 524304 | tf_op jit(solution)/shard_map/reduce_scatter | solution.py:39
  98.7 22.4 %psum.84 = f32[]{:T(128)} all-reduce(f32[]{:T(128)} %get-tuple-element.29), channel_id=1, replica_groups=mesh['rows'=2,'terms'=4] {'rows','terms'}, use_global_device_ids=true, to_apply=%region_3.0 | all-reduce | flops 1 | bytes 8 | tf_op jit(solution)/shard_map/psum | solution.py:40
  123.8 24.3 %psum.85 = f32[]{:T(128)} all-reduce(f32[]{:T(128)} %multiply_reduce_fusion.11), channel_id=1, replica_groups=mesh['rows'=2,'terms'=4] {'rows','terms'}, use_global_device_ids=true, to_apply=%region_5.0 | all-reduce | flops 1 | bytes 8 | tf_op jit(solution)/shard_map/psum | solution.py:42
  151.0 8.2 all_gather.30
  160.4 20.5 %all-gather.6.cloned.1.call-done = bf16[256,16,256]{2,1,0:T(8,128)(2,1)} async-done(((bf16[64,16,256]{2,1,0:T(8,128)(2,1)}), bf16[256,16,256]{2,1,0:T(8,128)(2,1)}) %all-gather.6.cloned.1.call-update) | async-done | bytes 2097168 | tf_op jit(solution)/shard_map/all_gather | solution.py:50
  180.8 11.0 %convert_bitcast_fusion.9 = bf16[16,256,16,128]{3,1,0,2:T(8,128)(2,1)} fusion(bf16[256,16,256,1]{2,1,0,3:T(8,128)(2,1)} %bitcast.149, bf16[16,128,256]{2,1,0:T(8,128)(2,1)S(1)} %copy-done.1), kind=kOutput, calls=%fused_computation.33 | convolution fusion | flops 4303355904 | bytes 19922944 | tf_op jit(solution)/shard_map/cpe,kbe->kcpb/dot_general | solution.py:10
  191.8 19.8 %convert_bitcast_fusion.8 = bf16[16,256,16,128]{3,2,1,0:T(8,128)(2,1)} fusion(bf16[16,256,16,128]{3,1,0,2:T(8,128)(2,1)} %convert_bitcast_fusion.9, bf16[16,16,16]{2,1,0:T(8,128)(2,1)S(1)} %copy-done.8), kind=kOutput, calls=%fused_computation.32 | convolution fusion | flops 276824064 | bytes 33562624 | tf_op jit(solution)/shard_map/kqp,kcpb->kcqb/dot_general | solution.py:11
  211.6 15.7 %fusion.54 = f32[256,16,128]{0,2,1:T(8,128)} fusion(bf16[16,256,256]{2,1,0:T(8,128)(2,1)S(1)} %copy-done, bf16[16,256,16,128]{3,2,1,0:T(8,128)(2,1)} %convert_bitcast_fusion.8), kind=kOutput, calls=%fused_computation.52 | convolution fusion | flops 4294967296 | bytes 20971520 | tf_op jit(solution)/shard_map/kac,kcqb->aqb/dot_general | solution.py:12
  230.5 25.6 %reduce-scatter.9.cloned.1.call-done = f32[64,16,128]{2,1,0:T(8,128)} async-done(((f32[256,16,128]{2,1,0:T(8,128)}), f32[64,16,128]{2,1,0:T(8,128)}) %reduce-scatter.9.cloned.1.call-update) | async-done | bytes 524304 | tf_op jit(solution)/shard_map/reduce_scatter | solution.py:39
  258.1 22.4 %psum.86 = f32[]{:T(128)} all-reduce(f32[]{:T(128)} %multiply_reduce_fusion.10), channel_id=1, replica_groups=mesh['rows'=2,'terms'=4] {'rows','terms'}, use_global_device_ids=true, to_apply=%region_8.0 | all-reduce | flops 1 | bytes 8 | tf_op jit(solution)/shard_map/psum | solution.py:40
  284.2 24.3 %psum.87 = f32[]{:T(128)} all-reduce(f32[]{:T(128)} %get-tuple-element.25), channel_id=1, replica_groups=mesh['rows'=2,'terms'=4] {'rows','terms'}, use_global_device_ids=true, to_apply=%region_10.0 | all-reduce | flops 1 | bytes 8 | tf_op jit(solution)/shard_map/psum | solution.py:42
  311.2 8.2 all_gather.32
  320.5 20.5 %all-gather.8.cloned.1.call-done = bf16[256,16,256]{2,1,0:T(8,128)(2,1)} async-done(((bf16[64,16,256]{2,1,0:T(8,128)(2,1)}), bf16[256,16,256]{2,1,0:T(8,128)(2,1)}) %all-gather.8.cloned.1.call-update) | async-done | bytes 2097168 | tf_op jit(solution)/shard_map/all_gather | solution.py:50
  341.0 11.2 %convert_bitcast_fusion.7 = bf16[16,256,16,128]{3,1,0,2:T(8,128)(2,1)} fusion(bf16[256,16,256,1]{2,1,0,3:T(8,128)(2,1)} %bitcast.150, bf16[16,128,256]{2,1,0:T(8,128)(2,1)S(1)} %copy-done.1), kind=kOutput, calls=%fused_computation.31 | convolution fusion | flops 4303355904 | bytes 19922944 | tf_op jit(solution)/shard_map/cpe,kbe->kcpb/dot_general | solution.py:10
  352.2 19.8 %convert_bitcast_fusion.6 = bf16[16,256,16,128]{3,2,1,0:T(8,128)(2,1)} fusion(bf16[16,256,16,128]{3,1,0,2:T(8,128)(2,1)} %convert_bitcast_fusion.7, bf16[16,16,16]{2,1,0:T(8,128)(2,1)S(1)} %copy-done.8), kind=kOutput, calls=%fused_computation.30 | convolution fusion | flops 276824064 | bytes 33562624 | tf_op jit(solution)/shard_map/kqp,kcpb->kcqb/dot_general | solution.py:11
  372.1 15.7 %fusion.59 = f32[256,16,128]{0,2,1:T(8,128)} fusion(bf16[16,256,256]{2,1,0:T(8,128)(2,1)S(1)} %copy-done, bf16[16,256,16,128]{3,2,1,0:T(8,128)(2,1)} %convert_bitcast_fusion.6), kind=kOutput, calls=%fused_computation.53 | convolution fusion | flops 4294967296 | bytes 20971520 | tf_op jit(solution)/shard_map/kac,kcqb->aqb/dot_general | solution.py:12
  390.9 25.6 %reduce-scatter.11.cloned.1.call-done = f32[64,16,128]{2,1,0:T(8,128)} async-done(((f32[256,16,128]{2,1,0:T(8,128)}), f32[64,16,128]{2,1,0:T(8,128)}) %reduce-scatter.11.cloned.1.call-update) | async-done | bytes 524304 | tf_op jit(solution)/shard_map/reduce_scatter | solution.py:39
  418.5 22.4 %psum.88 = f32[]{:T(128)} all-reduce(f32[]{:T(128)} %multiply_reduce_fusion.8), channel_id=1, replica_groups=mesh['rows'=2,'terms'=4] {'rows','terms'}, use_global_device_ids=true, to_apply=%region_13.0 | all-reduce | flops 1 | bytes 8 | tf_op jit(solution)/shard_map/psum | solution.py:40
  444.5 24.3 %psum.89 = f32[]{:T(128)} all-reduce(f32[]{:T(128)} %get-tuple-element.21), channel_id=1, replica_groups=mesh['rows'=2,'terms'=4] {'rows','terms'}, use_global_device_ids=true, to_apply=%region_15.0 | all-reduce | flops 1 | bytes 8 | tf_op jit(solution)/shard_map/psum | solution.py:42
  471.5 8.2 all_gather.34
  480.9 20.5 %all-gather.10.cloned.1.call-done = bf16[256,16,256]{2,1,0:T(8,128)(2,1)} async-done(((bf16[64,16,256]{2,1,0:T(8,128)(2,1)}), bf16[256,16,256]{2,1,0:T(8,128)(2,1)}) %all-gather.10.cloned.1.call-update) | async-done | bytes 2097168 | tf_op jit(solution)/shard_map/all_gather | solution.py:50
  501.3 11.0 %convert_bitcast_fusion.5 = bf16[16,256,16,128]{3,1,0,2:T(8,128)(2,1)} fusion(bf16[256,16,256,1]{2,1,0,3:T(8,128)(2,1)} %bitcast.151, bf16[16,128,256]{2,1,0:T(8,128)(2,1)S(1)} %copy-done.1), kind=kOutput, calls=%fused_computation.29 | convolution fusion | flops 4303355904 | bytes 19922944 | tf_op jit(solution)/shard_map/cpe,kbe->kcpb/dot_general | solution.py:10
  512.3 19.8 %convert_bitcast_fusion.4 = bf16[16,256,16,128]{3,2,1,0:T(8,128)(2,1)} fusion(bf16[16,256,16,128]{3,1,0,2:T(8,128)(2,1)} %convert_bitcast_fusion.5, bf16[16,16,16]{2,1,0:T(8,128)(2,1)S(1)} %copy-done.8), kind=kOutput, calls=%fused_computation.28 | convolution fusion | flops 276824064 | bytes 33562624 | tf_op jit(solution)/shard_map/kqp,kcpb->kcqb/dot_general | solution.py:11
  532.1 15.7 %fusion.64 = f32[256,16,128]{0,2,1:T(8,128)} fusion(bf16[16,256,256]{2,1,0:T(8,128)(2,1)S(1)} %copy-done, bf16[16,256,16,128]{3,2,1,0:T(8,128)(2,1)} %convert_bitcast_fusion.4), kind=kOutput, calls=%fused_computation.54 | convolution fusion | flops 4294967296 | bytes 20971520 | tf_op jit(solution)/shard_map/kac,kcqb->aqb/dot_general | solution.py:12
  551.1 25.6 %reduce-scatter.13.cloned.1.call-done = f32[64,16,128]{2,1,0:T(8,128)} async-done(((f32[256,16,128]{2,1,0:T(8,128)}), f32[64,16,128]{2,1,0:T(8,128)}) %reduce-scatter.13.cloned.1.call-update) | async-done | bytes 524304 | tf_op jit(solution)/shard_map/reduce_scatter | solution.py:39
  578.7 22.4 %psum.90 = f32[]{:T(128)} all-reduce(f32[]{:T(128)} %multiply_reduce_fusion.6), channel_id=1, replica_groups=mesh['rows'=2,'terms'=4] {'rows','terms'}, use_global_device_ids=true, to_apply=%region_18.0 | all-reduce | flops 1 | bytes 8 | tf_op jit(solution)/shard_map/psum | solution.py:40
  604.7 24.3 %psum.91 = f32[]{:T(128)} all-reduce(f32[]{:T(128)} %get-tuple-element.17), channel_id=1, replica_groups=mesh['rows'=2,'terms'=4] {'rows','terms'}, use_global_device_ids=true, to_apply=%region_20.0 | all-reduce | flops 1 | bytes 8 | tf_op jit(solution)/shard_map/psum | solution.py:42
  631.7 8.2 all_gather.36
  641.0 20.5 %all-gather.12.cloned.1.call-done = bf16[256,16,256]{2,1,0:T(8,128)(2,1)} async-done(((bf16[64,16,256]{2,1,0:T(8,128)(2,1)}), bf16[256,16,256]{2,1,0:T(8,128)(2,1)}) %all-gather.12.cloned.1.call-update) | async-done | bytes 2097168 | tf_op jit(solution)/shard_map/all_gather | solution.py:50
  661.5 11.2 %convert_bitcast_fusion.3 = bf16[16,256,16,128]{3,1,0,2:T(8,128)(2,1)} fusion(bf16[256,16,256,1]{2,1,0,3:T(8,128)(2,1)} %bitcast.152, bf16[16,128,256]{2,1,0:T(8,128)(2,1)S(1)} %copy-done.1), kind=kOutput, calls=%fused_computation.27 | convolution fusion | flops 4303355904 | bytes 19922944 | tf_op jit(solution)/shard_map/cpe,kbe->kcpb/dot_general | solution.py:10
  672.7 19.8 %convert_bitcast_fusion.2 = bf16[16,256,16,128]{3,2,1,0:T(8,128)(2,1)} fusion(bf16[16,256,16,128]{3,1,0,2:T(8,128)(2,1)} %convert_bitcast_fusion.3, bf16[16,16,16]{2,1,0:T(8,128)(2,1)S(1)} %copy-done.8), kind=kOutput, calls=%fused_computation.26 | convolution fusion | flops 276824064 | bytes 33562624 | tf_op jit(solution)/shard_map/kqp,kcpb->kcqb/dot_general | solution.py:11
  692.6 15.7 %fusion.69 = f32[256,16,128]{0,2,1:T(8,128)} fusion(bf16[16,256,256]{2,1,0:T(8,128)(2,1)S(1)} %copy-done, bf16[16,256,16,128]{3,2,1,0:T(8,128)(2,1)} %convert_bitcast_fusion.2), kind=kOutput, calls=%fused_computation.55 | convolution fusion | flops 4294967296 | bytes 20971520 | tf_op jit(solution)/shard_map/kac,kcqb->aqb/dot_general | solution.py:12
  711.4 25.6 %reduce-scatter.15.cloned.1.call-done = f32[64,16,128]{2,1,0:T(8,128)} async-done(((f32[256,16,128]{2,1,0:T(8,128)}), f32[64,16,128]{2,1,0:T(8,128)}) %reduce-scatter.15.cloned.1.call-update) | async-done | bytes 524304 | tf_op jit(solution)/shard_map/reduce_scatter | solution.py:39
  739.0 22.4 %psum.92 = f32[]{:T(128)} all-reduce(f32[]{:T(128)} %multiply_reduce_fusion.4), channel_id=1, replica_groups=mesh['rows'=2,'terms'=4] {'rows','terms'}, use_global_device_ids=true, to_apply=%region_23.0 | all-reduce | flops 1 | bytes 8 | tf_op jit(solution)/shard_map/psum | solution.py:40
  765.0 24.3 %psum.93 = f32[]{:T(128)} all-reduce(f32[]{:T(128)} %get-tuple-element.13), channel_id=1, replica_groups=mesh['rows'=2,'terms'=4] {'rows','terms'}, use_global_device_ids=true, to_apply=%region_25.0 | all-reduce | flops 1 | bytes 8 | tf_op jit(solution)/shard_map/psum | solution.py:42
  792.0 8.2 all_gather.38
  801.4 20.5 %all-gather.14.cloned.1.call-done = bf16[256,16,256]{2,1,0:T(8,128)(2,1)} async-done(((bf16[64,16,256]{2,1,0:T(8,128)(2,1)}), bf16[256,16,256]{2,1,0:T(8,128)(2,1)}) %all-gather.14.cloned.1.call-update) | async-done | bytes 2097168 | tf_op jit(solution)/shard_map/all_gather | solution.py:50
  821.9 11.0 %convert_bitcast_fusion.1 = bf16[16,256,16,128]{3,1,0,2:T(8,128)(2,1)} fusion(bf16[256,16,256,1]{2,1,0,3:T(8,128)(2,1)} %bitcast.153, bf16[16,128,256]{2,1,0:T(8,128)(2,1)S(1)} %copy-done.1), kind=kOutput, calls=%fused_computation.25 | convolution fusion | flops 4303355904 | bytes 19922944 | tf_op jit(solution)/shard_map/cpe,kbe->kcpb/dot_general | solution.py:10
  832.8 19.8 %convert_bitcast_fusion = bf16[16,256,16,128]{3,2,1,0:T(8,128)(2,1)} fusion(bf16[16,256,16,128]{3,1,0,2:T(8,128)(2,1)} %convert_bitcast_fusion.1, bf16[16,16,16]{2,1,0:T(8,128)(2,1)S(1)} %copy-done.8), kind=kOutput, calls=%fused_computation.24 | convolution fusion | flops 276824064 | bytes 33562624 | tf_op jit(solution)/shard_map/kqp,kcpb->kcqb/dot_general | solution.py:11
  852.7 15.7 %fusion.74 = f32[256,16,128]{0,2,1:T(8,128)} fusion(bf16[16,256,256]{2,1,0:T(8,128)(2,1)S(1)} %copy-done, bf16[16,256,16,128]{3,2,1,0:T(8,128)(2,1)} %convert_bitcast_fusion), kind=kOutput, calls=%fused_computation.56 | convolution fusion | flops 4294967296 | bytes 20971520 | tf_op jit(solution)/shard_map/kac,kcqb->aqb/dot_general | solution.py:12
  878.0 19.3 %reduce-scatter.17.cloned.1.call-done = f32[64,16,128]{2,1,0:T(8,128)} async-done(((f32[256,16,128]{2,1,0:T(8,128)}), f32[64,16,128]{2,1,0:T(8,128)}) %reduce-scatter.17.cloned.1.call-update) | async-done | bytes 524304 | tf_op jit(solution)/shard_map/reduce_scatter | solution.py:39
  900.1 22.4 %psum.94 = f32[]{:T(128)} all-reduce(f32[]{:T(128)} %multiply_reduce_fusion.2), channel_id=1, replica_groups=mesh['rows'=2,'terms'=4] {'rows','terms'}, use_global_device_ids=true, to_apply=%region_28.0 | all-reduce | flops 1 | bytes 8 | tf_op jit(solution)/shard_map/psum | solution.py:40
  925.9 24.3 %psum.95 = f32[]{:T(128)} all-reduce(f32[]{:T(128)} %get-tuple-element.9), channel_id=1, replica_groups=mesh['rows'=2,'terms'=4] {'rows','terms'}, use_global_device_ids=true, to_apply=%region_30.0 | all-reduce | flops 1 | bytes 8 | tf_op jit(solution)/shard_map/psum | solution.py:42
  952.8 6.2 copy.64
  (80 shorter events, 81.5 us)
Async XLA Ops:
  7.2 41.5 %copy-start = (bf16[16,256,256]{2,1,0:T(8,128)(2,1)S(1)}, bf16[16,256,256]{2,1,0:T(8,128)(2,1)}, u32[]{:S(2)}) copy-start(bf16[16,256,256]{2,1,0:T(8,128)(2,1)} %param.5) | copy-start | bytes 6291460
  7.2 88.7 %reduce-scatter.7.cloned.1.call-start = ((), (), s32[]{:S(2)}) async-start(), calls=%async_computation.6 | async-start | bytes 2621440 | tf_op jit(solution)/shard_map/reduce_scatter | solution.py:39
  15.7 4.5 copy-start.1
  18.1 2.0 copy-start.2
  20.2 8.6 copy-start.8
  67.4 113.4 %all-gather.6.cloned.1.call-start = ((), (), s32[]{:S(2)}) async-start(), calls=%async_computation.7 | async-start | bytes 2621440 | tf_op jit(solution)/shard_map/all_gather | solution.py:50
  160.3 95.9 %reduce-scatter.9.cloned.1.call-start = ((), (), s32[]{:S(2)}) async-start(), calls=%async_computation.8 | async-start | bytes 2621440 | tf_op jit(solution)/shard_map/reduce_scatter | solution.py:39
  230.5 110.5 %all-gather.8.cloned.1.call-start = ((), (), s32[]{:S(2)}) async-start(), calls=%async_computation.9 | async-start | bytes 2621440 | tf_op jit(solution)/shard_map/all_gather | solution.py:50
  320.5 96.0 %reduce-scatter.11.cloned.1.call-start = ((), (), s32[]{:S(2)}) async-start(), calls=%async_computation.10 | async-start | bytes 2621440 | tf_op jit(solution)/shard_map/reduce_scatter | solution.py:39
  390.8 110.5 %all-gather.10.cloned.1.call-start = ((), (), s32[]{:S(2)}) async-start(), calls=%async_computation.11 | async-start | bytes 2621440 | tf_op jit(solution)/shard_map/all_gather | solution.py:50
  480.8 95.9 %reduce-scatter.13.cloned.1.call-start = ((), (), s32[]{:S(2)}) async-start(), calls=%async_computation.12 | async-start | bytes 2621440 | tf_op jit(solution)/shard_map/reduce_scatter | solution.py:39
  551.0 110.5 %all-gather.12.cloned.1.call-start = ((), (), s32[]{:S(2)}) async-start(), calls=%async_computation.13 | async-start | bytes 2621440 | tf_op jit(solution)/shard_map/all_gather | solution.py:50
  641.0 96.0 %reduce-scatter.15.cloned.1.call-start = ((), (), s32[]{:S(2)}) async-start(), calls=%async_computation.14 | async-start | bytes 2621440 | tf_op jit(solution)/shard_map/reduce_scatter | solution.py:39
  711.3 110.5 %all-gather.14.cloned.1.call-start = ((), (), s32[]{:S(2)}) async-start(), calls=%async_computation.15 | async-start | bytes 2621440 | tf_op jit(solution)/shard_map/all_gather | solution.py:50
  801.3 95.9 %reduce-scatter.17.cloned.1.call-start = ((), (), s32[]{:S(2)}) async-start(), calls=%async_computation.16 | async-start | bytes 2621440 | tf_op jit(solution)/shard_map/reduce_scatter | solution.py:39
  868.4 3.2 copy-start.3
  868.4 4.0 copy-start.4
  871.6 5.6 copy-start.5
  872.4 50.7 %copy-start.6 = (f32[64,16,128]{2,0,1:T(8,128)S(1)}, f32[64,16,128]{2,0,1:T(8,128)}, u32[]{:S(2)}) copy-start(f32[64,16,128]{2,0,1:T(8,128)} %get-tuple-element.16) | copy-start | bytes 1572868
  873.3 26.0 %copy-start.7 = (f32[64,16,128]{2,0,1:T(8,128)S(1)}, f32[64,16,128]{2,0,1:T(8,128)}, u32[]{:S(2)}) copy-start(f32[64,16,128]{2,0,1:T(8,128)} %get-tuple-element.12) | copy-start | bytes 1572868
Sparse Core Ops, SparseCore 0:
  67.5 28.3 reduce-scatter.6
  160.4 20.3 all-gather.5
  230.6 25.5 reduce-scatter.8
  320.6 20.3 all-gather.7
  391.0 25.5 reduce-scatter.10
  480.9 20.3 all-gather.9
  551.1 25.5 reduce-scatter.12
  641.1 20.3 all-gather.11
  711.5 25.5 reduce-scatter.14
  801.5 20.3 all-gather.13
  871.7 25.5 reduce-scatter.16
where the time goes:
time: 973 us; the launch traced here: 967 us
  blocking collectives  322 us (33%)
  matrix products  277 us (28%)
  waiting for transfers between devices  253 us (26%)
  other arithmetic  48.1 us (5%)
  local copies, waits for them, and re-layouts  44.1 us (5%)
  between operations  23 us (2%)
    reduce_scatter x6, waiting for transfers between devices, body_fn(): lax.psum_scatter(part_sigma, 'terms', scatter_dimension=0, tiled=True)  150 us
    psum x6, blocking collectives, body_fn(): lax.psum(jnp.sum(w_vec * w_vec), ('rows', 'terms')) / elem_count  146 us
    psum x6, blocking collectives, body_fn(): lax.psum(jnp.sum(w_vec * cur_vec), ('rows', 'terms')) / elem_count  135 us
    dot_general x6, matrix products, local_sigma(): jnp.einsum('kqp,kcpb->kcqb', two_loc, right_part, preferred_element_type=...  119 us
    all_gather x5, waiting for transfers between devices, body_fn(): full_u = lax.all_gather(col_gather, 'terms', axis=0, tiled=True)  102 us
    dot_general x6, matrix products, local_sigma(): jnp.einsum('kac,kcqb->aqb', left_loc, mid_part, preferred_element_type=jn...  94.2 us
    dot_general x6, matrix products, local_sigma(): jnp.einsum('cpe,kbe->kcpb', full_u, right_loc, preferred_element_type=jnp...  64.1 us
    all_gather x5, blocking collectives, body_fn(): lax.all_gather(next_vec.astype(jnp.bfloat16), 'rows', axis=2, tiled=True)  40.9 us
  transfers between devices with their start and end apart: 11, of which 11 were waited for; matrix products, arithmetic and copies ran while one was open for 1% of the time, Pallas kernels for 0%

commit v1 on v0

v1 whole, which is shorter than its diff:
```python
import functools

import jax
import jax.numpy as jnp
from jax import lax
from jax.experimental import pallas as pl
from jax.experimental.pallas import tpu as pltpu
from jax.sharding import PartitionSpec as P

STEPS = 6
PAIR = 16
BOND = 256
TERMS = 64
GROUP = 8
NGROUPS = TERMS // GROUP
HALF = 128
QUART = 64
ELEMS = float(BOND * BOND * PAIR)
F32 = jnp.float32
BF16 = jnp.bfloat16


def lanczos_kernel(
    wf_hbm, left_hbm, two_ref, right_hbm, kry_hbm, ab_ref,
    wfv, rw, lw, bd, wt, mask, yb, zb, uT, acc, rbuf, vb, tmp, st, betas, xs, xr, osb,
    loc_sem, w_ssem, w_rsem, r_ssem, r_rsem, l_ssem, l_rsem, fw_ssem,
    u_ssem, u_rsem, p_ssem, p_rsem, st_ssem, st_rsem, x_ssem, x_rsem, o_sem,
):
    y = lax.axis_index("rows")
    t = lax.axis_index("terms")
    x = t // 2
    c = t % 2
    me = y * 4 + t
    bq = 2 * y + x
    sib = (y, 2 * x + (1 - c))
    xnb = (y, 2 * (1 - x) + c)
    xno = (y, 2 * (1 - x) + (1 - c))
    ynb = (1 - y, t)
    diag = (1 - y, 2 * (1 - x) + c)

    def rdma(src, dst, ssem, rsem, dev):
        return pltpu.make_async_remote_copy(
            src_ref=src, dst_ref=dst, send_sem=ssem, recv_sem=rsem,
            device_id=dev, device_id_type=pl.DeviceIdType.MESH)

    cp_wf = pltpu.make_async_copy(wf_hbm, wfv, loc_sem.at[0])
    cp_r = pltpu.make_async_copy(right_hbm.at[:, pl.ds(64 * x, 64), :], rw.at[pl.ds(0, 16)], loc_sem.at[1])
    cp_l = pltpu.make_async_copy(left_hbm.at[:, pl.ds(128 * c, 128), :], lw.at[pl.ds(0, 16)], loc_sem.at[2])
    cp_wf.start()
    cp_r.start()
    cp_l.start()

    barrier = pltpu.get_barrier_semaphore()
    for q in range(1, 8):
        d = (me + q) % 8
        pl.semaphore_signal(barrier, inc=1, device_id=(d // 4, d % 4), device_id_type=pl.DeviceIdType.MESH)
    pl.semaphore_wait(barrier, 7)

    def l_sib():
        return rdma(left_hbm.at[:, pl.ds(128 * (1 - c), 128), :], lw.at[pl.ds(16, 16)], l_ssem.at[0], l_rsem.at[0], sib)

    def l_dir(i):
        rows = pl.ds(128 * c, 128) if i == 0 else pl.ds(128 * (1 - c), 128)
        return rdma(left_hbm.at[pl.ds(8 * y, 8), rows, :], lw.at[pl.ds(32 + 8 * i, 8)],
                    l_ssem.at[1 + i], l_rsem.at[1 + i], xnb if i == 0 else xno)

    def l_fwd(i):
        return rdma(lw.at[pl.ds(32 + 8 * i, 8)], lw.at[pl.ds(48 + 8 * i, 8)], l_ssem.at[3 + i], l_rsem.at[3 + i], ynb)

    def r_sib():
        return rdma(right_hbm.at[:, pl.ds(64 * x, 64), :], rw.at[pl.ds(16, 16)], r_ssem.at[0], r_rsem.at[0], sib)

    def r_dir(i):
        first = 8 * y if i == 0 else 8 * (1 - y)
        return rdma(right_hbm.at[pl.ds(first, 8), pl.ds(64 * (1 - x), 64), :], rw.at[pl.ds(32 + 16 * i, 8)],
                    r_ssem.at[1 + i], r_rsem.at[1 + i], xnb)

    def r_fwd(i):
        return rdma(rw.at[pl.ds(32 + 16 * i, 8)], rw.at[pl.ds(40 + 16 * i, 8)], r_ssem.at[3 + i], r_rsem.at[3 + i], sib)

    l_dir(0).start()
    l_dir(1).start()
    r_dir(0).start()
    r_dir(1).start()
    r_sib().start()
    l_sib().start()

    row16 = lax.broadcasted_iota(jnp.int32, (PAIR, BOND), 0)
    lane16 = lax.broadcasted_iota(jnp.int32, (PAIR, BOND), 1)
    packed = jnp.zeros((PAIR, BOND), F32)
    for k in range(16):
        place = (lane16 == row16 + 16 * k).astype(F32).astype(BF16)
        packed = packed + jnp.dot(two_ref[k], place, preferred_element_type=F32)
    wt[0] = packed.astype(BF16)

    def w_send(i):
        return rdma(wt.at[0], wt.at[1 + i], w_ssem.at[i], w_rsem.at[i], (sib, xnb, xno)[i])

    for i in range(3):
        w_send(i).start()

    rr = lax.broadcasted_iota(jnp.int32, (BOND, BOND), 0) % 16
    cc = lax.broadcasted_iota(jnp.int32, (BOND, BOND), 1) % 16
    mask[...] = (rr == cc).astype(F32)

    cp_wf.wait()

    def sumsq(i, s):
        blk = wfv[pl.ds(pl.multiple_of(i * 256, 256), 256), :]
        return s + jnp.sum((blk * blk).reshape(32, 8, 128), axis=0)

    total = lax.fori_loop(0, 32, sumsq, jnp.zeros((8, 128), F32))
    total = jnp.sum(jnp.sum(total, axis=1, keepdims=True), axis=0, keepdims=True)
    scale = jnp.broadcast_to(jnp.sqrt(total * (1.0 / ELEMS)), (1, 128))

    wfh = wfv.at[pl.ds(pl.multiple_of(4096 * c, 4096), 4096), :]
    wfo = wfv.at[pl.ds(pl.multiple_of(2048 * t, 2048), 2048), :]
    for p in range(PAIR):
        for bt in range(2):
            first = (p // 4) * 8 + bt * 4 + p % 4
            blk = (wfh[pl.ds(first, 128, stride=32), :] / scale).T
            tmp[bt] = blk
            uT[p, pl.ds(128 * bt, 128), :] = blk.astype(BF16)
        vb[0, p] = tmp[y, pl.ds(pl.multiple_of(64 * x, 64), 64), :]
        first = (p // 4) * 8 + p % 4
        lo = wfo[pl.ds(first, 64, stride=32), :]
        hi = wfo[pl.ds(first + 4, 64, stride=32), :]
        osb[p] = jnp.where(y == 0, lo, hi) / scale
    vb[2] = jnp.zeros((PAIR, QUART, HALF), F32)
    betas[...] = jnp.zeros((1, 128), F32)

    def out_copy(j):
        return pltpu.make_async_copy(osb, kry_hbm.at[j], o_sem.at[0])

    out_copy(0).start()

    def u_copy(n, s):
        part = uT.at[pl.ds(2 * n, 2), pl.ds(pl.multiple_of(64 * bq, 64), 64), :]
        return rdma(part, part, u_ssem.at[n, s], u_rsem.at[n, s], (xnb, ynb, diag)[s])

    def u_wait_recv(n, s):
        src = (2 * y + (1 - x), 2 * (1 - y) + x, 2 * (1 - y) + (1 - x))[s]
        part = uT.at[pl.ds(2 * n, 2), pl.ds(pl.multiple_of(64 * src, 64), 64), :]
        rdma(part, part, u_ssem.at[n, s], u_rsem.at[n, s], (xnb, ynb, diag)[s]).wait_recv()

    def r_stage(k0, nk, n):
        lhs = rw[pl.ds(k0, nk)].reshape(nk * QUART, BOND)
        rhs = jnp.concatenate([uT[2 * n], uT[2 * n + 1]], axis=1)
        res = jnp.dot(lhs, rhs, preferred_element_type=F32).astype(BF16)
        yb[pl.ds(k0, nk), 2 * n] = res[:, :HALF].reshape(nk, QUART, HALF)
        yb[pl.ds(k0, nk), 2 * n + 1] = res[:, HALF:].reshape(nk, QUART, HALF)

    def wl_stage(g):
        k0 = g * GROUP
        for k in range(GROUP):
            mat = bd[k0 + k]
            for h in range(2):
                rhs = jnp.concatenate(
                    [yb[k0 + k, :, pl.ds(32 * h + 16 * i, 16), :].reshape(BOND, HALF) for i in range(2)], axis=1)
                res = jnp.dot(mat, rhs, preferred_element_type=F32).astype(BF16)
                for i in range(2):
                    zb[:, pl.ds(32 * h + 16 * i, 16), pl.ds(HALF * k, HALF)] = (
                        res[:, HALF * i:HALF * (i + 1)].reshape(PAIR, 16, HALF))
        lhs = zb[...].reshape(PAIR * QUART, GROUP * HALF)
        rhs = lw[pl.ds(k0, GROUP)].reshape(GROUP * HALF, BOND)
        res = jnp.dot(lhs, rhs, preferred_element_type=F32)
        acc[0] = acc[0] + res[:, :HALF].reshape(PAIR, QUART, HALF)
        acc[1] = acc[1] + res[:, HALF:].reshape(PAIR, QUART, HALF)

    def build_bd(g):
        slot = (g // 4) * 2 + (1 - g // 4) * (g // 2) + (g // 4) * (g % 2)
        part = (1 - g // 4) * (g % 2) + (g // 4) * ((y + (g - 4 * (g // 4)) // 2) % 2)
        lanes = pl.multiple_of(128 * part, 128)
        ops = wt[slot, :, pl.ds(lanes, 128)].astype(F32).T.astype(BF16)
        e_t = (lax.broadcasted_iota(jnp.int32, (PAIR, BOND), 1) // 16
               == lax.broadcasted_iota(jnp.int32, (PAIR, BOND), 0)).astype(F32).astype(BF16)
        e = (lax.broadcasted_iota(jnp.int32, (BOND, PAIR), 0) // 16
             == lax.broadcasted_iota(jnp.int32, (BOND, PAIR), 1)).astype(F32).astype(BF16)
        wide = jnp.dot(ops, e_t, preferred_element_type=F32).astype(BF16)
        for k in range(GROUP):
            full = jnp.dot(e, wide[16 * k:16 * (k + 1), :], preferred_element_type=F32)
            bd[g * GROUP + k] = (full * mask[...]).astype(BF16)

    def first_group(g, carry):
        @pl.when(g == 0)
        def _():
            cp_r.wait()
            cp_l.wait()

        @pl.when(g == 2)
        def _():
            w_send(0).wait_recv()
            r_sib().wait_recv()
            l_sib().wait_recv()

        @pl.when(g == 4)
        def _():
            w_send(1).wait_recv()
            w_send(2).wait_recv()
            l_dir(0).wait_recv()
            l_fwd(0).start()
            l_dir(1).wait_recv()
            l_fwd(1).start()
            r_dir(0).wait_recv()
            r_fwd(0).start()

        @pl.when(g == 5)
        def _():
            r_fwd(0).wait_recv()

        @pl.when(g == 6)
        def _():
            r_dir(1).wait_recv()
            r_fwd(1).start()
            l_fwd(0).wait_recv()

        @pl.when(g == 7)
        def _():
            r_fwd(1).wait_recv()
            l_fwd(1).wait_recv()

        build_bd(g)
        for n in range(8):
            r_stage(g * GROUP, GROUP, n)
        wl_stage(g)
        return carry

    def later_r(n, carry):
        for s in range(3):
            u_wait_recv(n, s)
        for i in range(4):
            r_stage(16 * i, 16, n)
        for s in range(3):
            u_copy(n, s).wait_send()
        return carry

    def later_wl(g, carry):
        wl_stage(g)
        return carry

    def part_copy():
        return rdma(acc.at[1 - c], rbuf, p_ssem.at[0], p_rsem.at[0], sib)

    def x_copy(par, h):
        return rdma(xs.at[h], xr.at[par, x], x_ssem.at[h], x_rsem.at[par, x], (y, 2 * c + h))

    def x_recv(par, slot):
        rdma(xs.at[0], xr.at[par, slot], x_ssem.at[0], x_rsem.at[par, slot], xnb).wait_recv()

    def x_wait_send(par):
        @pl.when(c == x)
        def _():
            x_copy(par, 1 - c).wait_send()

        @pl.when(c != x)
        def _():
            x_copy(par, 0).wait_send()
            x_copy(par, 1).wait_send()

    def put_out(vec, par):
        for i in range(8):
            blk = jnp.concatenate([vb[vec, i], vb[vec, i + 8]], axis=0).T
            xs[0, i] = blk[:64]
            xs[1, i] = blk[64:]

        @pl.when(c == x)
        def _():
            xr[par, x] = xs[c]
            x_copy(par, 1 - c).start()

        @pl.when(c != x)
        def _():
            x_copy(par, 0).start()
            x_copy(par, 1).start()

    def merge_out(j, par):
        x_recv(par, 1 - x)

        @pl.when(c != x)
        def _():
            x_recv(par, x)

        out_copy(0).wait()
        low = lax.broadcasted_iota(jnp.int32, (64, 128), 1) < 64
        for i in range(8):
            p0 = xr[par, 0, i]
            p1 = xr[par, 1, i]
            osb[i] = jnp.where(low, p0, pltpu.roll(p1, 64, 1))
            osb[i + 8] = jnp.where(low, pltpu.roll(p0, 64, 1), p1)
        out_copy(j).start()

    def everywhere(s):
        s = jnp.sum(jnp.sum(s, axis=1, keepdims=True), axis=0, keepdims=True)
        return jnp.broadcast_to(s, (1, 128))

    def fold(v):
        return jnp.sum(v.reshape(8, 8, 128), axis=0)

    def step(j, carry):
        acc[...] = jnp.zeros((2, PAIR, QUART, HALF), F32)

        @pl.when(j == 0)
        def _():
            lax.fori_loop(0, NGROUPS, first_group, 0)

        @pl.when(j > 0)
        def _():
            lax.fori_loop(0, 8, later_r, 0)
            lax.fori_loop(0, NGROUPS, later_wl, 0)

        part_copy().start()
        cur = j % 3
        prev = (j + 2) % 3
        nxt = (j + 1) % 3
        par = j % 2
        beta_prev = betas[...]
        part_copy().wait_recv()

        zero = jnp.zeros((8, 128), F32)

        def pass1(p, s):
            a_s, t_s, v_s = s
            w = acc[c, p] + rbuf[p]
            v = vb[cur, p]
            r = w - beta_prev * vb[prev, p]
            vb[nxt, p] = r
            return a_s + fold(w * v), t_s + fold(r * v), v_s + fold(v * v)

        a_s, t_s, v_s = lax.fori_loop(0, PAIR, pass1, (zero, zero, zero))
        a_d, t_d, v_d = everywhere(a_s), everywhere(t_s), everywhere(v_s)
        shift = jnp.where(v_d > 0.0, t_d / jnp.where(v_d > 0.0, v_d, 1.0), 0.0)

        def pass2(p, s):
            q_s, p_s = s
            v = vb[cur, p]
            r = vb[nxt, p] - shift * v
            vb[nxt, p] = r
            return q_s + fold(r * r), p_s + fold(r * v)

        q_s, p_s = lax.fori_loop(0, PAIR, pass2, (zero, zero))
        st[par, me] = jnp.concatenate(
            [a_d, shift, v_d, everywhere(q_s), everywhere(p_s), jnp.zeros((3, 128), F32)], axis=0)

        def st_copy(q):
            d = (me + q) % 8
            return rdma(st.at[par, me], st.at[par, me], st_ssem.at[q - 1], st_rsem.at[q - 1], (d // 4, d % 4))

        for q in range(1, 8):
            st_copy(q).start()
        part_copy().wait_send()
        for q in range(1, 8):
            src = (me + 8 - q) % 8
            rdma(st.at[par, me], st.at[par, src], st_ssem.at[q - 1], st_rsem.at[q - 1], sib).wait_recv()

        alpha = st[par, 0][0:1]
        for d in range(1, 8):
            alpha = alpha + st[par, d][0:1]
        alpha = alpha * (1.0 / ELEMS)
        beta2 = jnp.zeros((1, 128), F32)
        for d in range(8):
            tile = st[par, d]
            gap = alpha - tile[1:2]
            beta2 = beta2 + (tile[3:4] - 2.0 * gap * tile[4:5] + gap * gap * tile[2:3])
        beta = jnp.sqrt(beta2 * (1.0 / ELEMS))
        betas[...] = beta
        ab_ref[j] = jnp.concatenate([alpha, beta, jnp.zeros((6, 128), F32)], axis=0)
        gap = alpha - shift

        def pass3(n, carry):
            for i in range(2):
                p = 2 * n + i
                v = (vb[nxt, p] - gap * vb[cur, p]) / beta
                vb[nxt, p] = v
                uT[p, pl.ds(pl.multiple_of(64 * bq, 64), 64), :] = v.astype(BF16)

            @pl.when(j < STEPS - 1)
            def _():
                for s in range(3):
                    u_copy(n, s).start()

            return carry

        lax.fori_loop(0, 8, pass3, 0)

        @pl.when(j > 0)
        def _():
            x_wait_send(1 - par)

        put_out(nxt, par)

        @pl.when(j > 0)
        def _():
            merge_out(j, 1 - par)

        for q in range(1, 8):
            st_copy(q).wait_send()
        return carry

    lax.fori_loop(0, STEPS, step, 0)

    last = (STEPS - 1) % 2
    x_wait_send(last)
    merge_out(STEPS, last)
    out_copy(0).wait()

    for i in range(3):
        w_send(i).wait_send()
    l_sib().wait_send()
    r_sib().wait_send()
    for i in range(2):
        l_dir(i).wait_send()
        l_fwd(i).wait_send()
        r_dir(i).wait_send()
        r_fwd(i).wait_send()


def solution(mesh):
    def body_fn(wavefunc, left_loc, two_loc, right_loc):
        bond, phys = wavefunc.shape[0], wavefunc.shape[1]
        wf = wavefunc.reshape(bond, phys, phys, 2, 128).transpose(0, 1, 3, 2, 4).reshape(-1, 128)
        dma = pltpu.SemaphoreType.DMA
        kry, ab = pl.pallas_call(
            lanczos_kernel,
            out_shape=(
                jax.ShapeDtypeStruct((STEPS + 1, PAIR, 64, 128), F32),
                jax.ShapeDtypeStruct((STEPS, 8, 128), F32),
            ),
            in_specs=[
                pl.BlockSpec(memory_space=pl.ANY),
                pl.BlockSpec(memory_space=pl.ANY),
                pl.BlockSpec(memory_space=pltpu.VMEM),
                pl.BlockSpec(memory_space=pl.ANY),
            ],
            out_specs=(pl.BlockSpec(memory_space=pl.ANY), pl.BlockSpec(memory_space=pltpu.VMEM)),
            scratch_shapes=[
                pltpu.VMEM((8192, 128), F32),
                pltpu.VMEM((TERMS, QUART, BOND), BF16),
                pltpu.VMEM((TERMS, HALF, BOND), BF16),
                pltpu.VMEM((TERMS, BOND, BOND), BF16),
                pltpu.VMEM((4, PAIR, BOND), BF16),
                pltpu.VMEM((BOND, BOND), F32),
                pltpu.VMEM((TERMS, PAIR, QUART, HALF), BF16),
                pltpu.VMEM((PAIR, QUART, GROUP * HALF), BF16),
                pltpu.VMEM((PAIR, BOND, HALF), BF16),
                pltpu.VMEM((2, PAIR, QUART, HALF), F32),
                pltpu.VMEM((PAIR, QUART, HALF), F32),
                pltpu.VMEM((3, PAIR, QUART, HALF), F32),
                pltpu.VMEM((2, 128, 128), F32),
                pltpu.VMEM((2, 8, 8, 128), F32),
                pltpu.VMEM((1, 128), F32),
                pltpu.VMEM((2, 8, 64, 128), F32),
                pltpu.VMEM((2, 2, 8, 64, 128), F32),
                pltpu.VMEM((PAIR, 64, 128), F32),
                dma((3,)),
                dma((3,)), dma((3,)),
                dma((5,)), dma((5,)),
                dma((5,)), dma((5,)),
                dma((1,)),
                dma((8, 3)), dma((8, 3)),
                dma((1,)), dma((1,)),
                dma((7,)), dma((7,)),
                dma((2,)), dma((2, 2)),
                dma((1,)),
            ],
            compiler_params=pltpu.CompilerParams(
                collective_id=0, has_side_effects=True, vmem_limit_bytes=66 * 1000 * 1000),
        )(wf, left_loc, two_loc, right_loc)
        krylov = kry.transpose(0, 2, 1, 3).reshape(STEPS + 1, 64, phys, phys, 128)
        return krylov, ab[:, 0, 0], ab[:, 1, 0]

    return jax.shard_map(
        body_fn, mesh=mesh,
        in_specs=(P(), P('terms'), P('terms'), P('terms', 'rows')),
        out_specs=(P(None, 'terms', None, None, 'rows'), P(), P()), check_vma=False)
```

time: 973 us -> 246 us (0.25)
  blocking collectives: 322 us -> 0 us
  matrix products: 277 us -> 0 us
  waiting for transfers between devices: 253 us -> 0 us
  Pallas kernels: 0 us -> 236 us
  other arithmetic: 48.1 us -> 0 us
  local copies, waits for them, and re-layouts: 44.1 us -> 7.69 us
  between operations: 23 us -> 0.64 us
    psum x12 -> x0, blocking collectives: 281 us -> none  [the longest x6 146 us: body_fn(): lax.psum(jnp.sum(w_vec * w_vec), ('rows', 'terms')) / elem_count]
    dot_general x18 -> x0, matrix products: 277 us -> none  [the longest x6 119 us: local_sigma(): jnp.einsum('kqp,kcpb->kcqb', two_loc, right_part, preferred_element_type=...]
    pallas_call x0 -> x1, Pallas kernels: none -> 236 us  [body_fn(): pl.pallas_call(lanczos_kernel, out_shape=(jax.ShapeDtypeStruct((STEPS + 1...]
    reduce_scatter x6 -> x0, waiting for transfers between devices: 150 us -> none  [body_fn(): lax.psum_scatter(part_sigma, 'terms', scatter_dimension=0, tiled=True)]
    all_gather x5 -> x0, waiting for transfers between devices: 102 us -> none  [body_fn(): full_u = lax.all_gather(col_gather, 'terms', axis=0, tiled=True)]
    all_gather x5 -> x0, blocking collectives: 40.9 us -> none  [body_fn(): lax.all_gather(next_vec.astype(jnp.bfloat16), 'rows', axis=2, tiled=True)]
    reduce_sum x13 -> x0, other arithmetic: 34.3 us -> none  [the longest x6 16.5 us: body_fn(): jnp.sum(w_vec * w_vec)]
    dot_general x6 -> x0, local copies, waits for them, and re-layouts: 18.6 us -> none  [local_sigma(): jnp.einsum('kac,kcqb->aqb', left_loc, mid_part, preferred_element_type=jn...]
  transfers between devices with their start and end apart: 11 -> 0, of which waited for: 11 -> 0; matrix products, arithmetic and copies ran while one was open for 1% -> 0% of each run, Pallas kernels for 0% -> 0%
where the time goes in v1:
time: 246 us; the launch traced here: 244 us
  Pallas kernels  236 us (96%)
  local copies, waits for them, and re-layouts  7.69 us (3%)
    pallas_call x1, Pallas kernels, body_fn(): pl.pallas_call(lanczos_kernel, out_shape=(jax.ShapeDtypeStruct((STEPS + 1...  236 us
    unnamed x1, local copies, waits for them, and re-layouts  6.24 us

profile of v1, /device:TPU:0, one launch (start us, length us, event | category | flops | bytes accessed | tf_op | source)
XLA Modules:
  0.0 244.1 jit_solution(11205453946616010450)
XLA Ops:
  0.6 235.8 %shard_map.67 = (f32[7,16,64,128]{3,2,1,0:T(8,128)}, f32[6,8,128]{2,1,0:T(8,128)}) custom-call(f32[8192,128]{1,0:T(8,128)} %bitcast.8, bf16[16,256,256]{2,1,0:T(8,128)(2,1)} %left_hbm.1, bf16[16,16,16]{2,1,0:T(8,128)(2,1)} %two_ref.1, bf16[16,128,256]{2,1,0:T(8,128)(2,1)} %right_hbm.1), custom_call_target="tpu_custom_call" | custom-call | tf_op jit(solution)/shard_map/pallas_call | solution.py:422
  236.4 1.5 slice_reduce_fusion
  237.9 6.2 %copy.10 = f32[7,64,4,4,128]{4,3,2,1,0:T(4,128)} copy(f32[7,64,4,4,128]{4,1,3,2,0:T(8,128)} %bitcast.9) | data formatting | bytes 7340032

commit v2 on v1

--- a/solution.py
+++ b/solution.py
@@ -15,6 +15,8 @@
 NGROUPS = TERMS // GROUP
 HALF = 128
 QUART = 64
+AHEAD = 3
+LAG = 2
 ELEMS = float(BOND * BOND * PAIR)
 F32 = jnp.float32
 BF16 = jnp.bfloat16
@@ -36,7 +38,6 @@
     xnb = (y, 2 * (1 - x) + c)
     xno = (y, 2 * (1 - x) + (1 - c))
     ynb = (1 - y, t)
-    diag = (1 - y, 2 * (1 - x) + c)
 
     def rdma(src, dst, ssem, rsem, dev):
         return pltpu.make_async_remote_copy(
@@ -134,14 +135,26 @@
 
     out_copy(0).start()
 
-    def u_copy(n, s):
-        part = uT.at[pl.ds(2 * n, 2), pl.ds(pl.multiple_of(64 * bq, 64), 64), :]
-        return rdma(part, part, u_ssem.at[n, s], u_rsem.at[n, s], (xnb, ynb, diag)[s])
-
-    def u_wait_recv(n, s):
-        src = (2 * y + (1 - x), 2 * (1 - y) + x, 2 * (1 - y) + (1 - x))[s]
-        part = uT.at[pl.ds(2 * n, 2), pl.ds(pl.multiple_of(64 * src, 64), 64), :]
-        rdma(part, part, u_ssem.at[n, s], u_rsem.at[n, s], (xnb, ynb, diag)[s]).wait_recv()
+    def u_part(n, quarter):
+        return uT.at[pl.ds(2 * n, 2), pl.ds(pl.multiple_of(64 * quarter, 64), 64), :]
+
+    def u_own(n, s):
+        part = u_part(n, bq)
+        return rdma(part, part, u_ssem.at[n, s], u_rsem.at[n, s], (xnb, ynb)[s])
+
+    def u_got(n, s):
+        part = u_part(n, (2 * y + (1 - x), 2 * (1 - y) + x)[s])
+        return rdma(part, part, u_ssem.at[n, s], u_rsem.at[n, s], (xnb, ynb)[s])
+
+    def u_fwd(n):
+        odd = n % 2
+        part = u_part(n, (1 - odd) * (2 * y + (1 - x)) + odd * (2 * (1 - y) + x))
+        dev = ((1 - odd) * (1 - y) + odd * y, 2 * ((1 - odd) * x + odd * (1 - x)) + c)
+        return rdma(part, part, u_ssem.at[n, 2], u_rsem.at[n, 2], dev)
+
+    def u_diag(n):
+        part = u_part(n, 2 * (1 - y) + (1 - x))
+        return rdma(part, part, u_ssem.at[n, 2], u_rsem.at[n, 2], xnb)
 
     def r_stage(k0, nk, n):
         lhs = rw[pl.ds(k0, nk)].reshape(nk * QUART, BOND)
@@ -225,13 +238,28 @@
         wl_stage(g)
         return carry
 
-    def later_r(n, carry):
-        for s in range(3):
-            u_wait_recv(n, s)
-        for i in range(4):
-            r_stage(16 * i, 16, n)
-        for s in range(3):
-            u_copy(n, s).wait_send()
+    def later_r(i, carry):
+        @pl.when(i < 8)
+        def _():
+            u_got(i, 0).wait_recv()
+            u_got(i, 1).wait_recv()
+            u_fwd(i).start()
+
+        @pl.when(i < 8 - AHEAD)
+        def _():
+            u_own(i + AHEAD, 0).start()
+            u_own(i + AHEAD, 1).start()
+
+        @pl.when(i >= LAG)
+        def _():
+            n = i - LAG
+            u_diag(n).wait_recv()
+            for k in range(4):
+                r_stage(16 * k, 16, n)
+            u_own(n, 0).wait_send()
+            u_own(n, 1).wait_send()
+            u_fwd(n).wait_send()
+
         return carry
 
     def later_wl(g, carry):
@@ -266,6 +294,10 @@
         @pl.when(c == x)
         def _():
             xr[par, x] = xs[c]
+
+    def x_start(par):
+        @pl.when(c == x)
+        def _():
             x_copy(par, 1 - c).start()
 
         @pl.when(c != x)
@@ -305,7 +337,8 @@
 
         @pl.when(j > 0)
         def _():
-            lax.fori_loop(0, 8, later_r, 0)
+            lax.fori_loop(0, 8 + LAG, later_r, 0)
+            x_start((j + 1) % 2)
             lax.fori_loop(0, NGROUPS, later_wl, 0)
 
         part_copy().start()
@@ -373,10 +406,10 @@
                 vb[nxt, p] = v
                 uT[p, pl.ds(pl.multiple_of(64 * bq, 64), 64), :] = v.astype(BF16)
 
-            @pl.when(j < STEPS - 1)
+            @pl.when((j < STEPS - 1) & (n < AHEAD))
             def _():
-                for s in range(3):
-                    u_copy(n, s).start()
+                u_own(n, 0).start()
+                u_own(n, 1).start()
 
             return carry
 
@@ -399,6 +432,7 @@
     lax.fori_loop(0, STEPS, step, 0)
 
     last = (STEPS - 1) % 2
+    x_start(last)
     x_wait_send(last)
     merge_out(STEPS, last)
     out_copy(0).wait()

time: 246 us -> 250 us (1.016)
  Pallas kernels: 236 us -> 240 us
    pallas_call x1, Pallas kernels: 236 us -> 240 us  [body_fn(): pl.pallas_call(lanczos_kernel, out_shape=(jax.ShapeDtypeStruct((STEPS + 1...]
where the time goes in v2:
time: 250 us; the launch traced here: 248 us
  Pallas kernels  240 us (96%)
  local copies, waits for them, and re-layouts  7.69 us (3%)
    pallas_call x1, Pallas kernels, body_fn(): pl.pallas_call(lanczos_kernel, out_shape=(jax.ShapeDtypeStruct((STEPS + 1...  240 us
    unnamed x1, local copies, waits for them, and re-layouts  6.24 us

profile of v2, /device:TPU:0, one launch (start us, length us, event | category | flops | bytes accessed | tf_op | source)
XLA Modules:
  0.0 248.2 jit_solution(12174553149558221815)
XLA Ops:
  0.6 239.8 %shard_map.67 = (f32[7,16,64,128]{3,2,1,0:T(8,128)}, f32[6,8,128]{2,1,0:T(8,128)}) custom-call(f32[8192,128]{1,0:T(8,128)} %bitcast.8, bf16[16,256,256]{2,1,0:T(8,128)(2,1)} %left_hbm.1, bf16[16,16,16]{2,1,0:T(8,128)(2,1)} %two_ref.1, bf16[16,128,256]{2,1,0:T(8,128)(2,1)} %right_hbm.1), custom_call_target="tpu_custom_call" | custom-call | tf_op jit(solution)/shard_map/pallas_call | solution.py:456
  240.5 1.5 slice_reduce_fusion
  241.9 6.2 %copy.10 = f32[7,64,4,4,128]{4,3,2,1,0:T(4,128)} copy(f32[7,64,4,4,128]{4,1,3,2,0:T(8,128)} %bitcast.9) | data formatting | bytes 7340032

commit v3 on v1

v3 whole, which is shorter than its diff:
```python
import jax
import jax.numpy as jnp
from jax import lax
from jax.experimental import pallas as pl
from jax.experimental.pallas import tpu as pltpu
from jax.sharding import PartitionSpec as P

STEPS = 6
PAIR = 16
BOND = 256
TERMS = 64
BLOCK = 16
HALF = 128
COLS = 32
ELEMS = float(BOND * BOND * PAIR)
F32 = jnp.float32
BF16 = jnp.bfloat16


def lanczos_kernel(
    wf_hbm, left_hbm, two_ref, right_hbm, kry_hbm, ab_ref,
    wfv, rw, lw, bd, wt, mask, yb, zb, uT, acc, vb, tmp, st, betas, xs, xr, osb,
    loc_sem, w_ssem, w_rsem, r_ssem, r_rsem, l_ssem, l_rsem, lx_ssem, lx_rsem,
    u_ssem, u_rsem, f_ssem, f_rsem, st_ssem, st_rsem, x_ssem, x_rsem, o_sem,
):
    y = lax.axis_index("rows")
    t = lax.axis_index("terms")
    x = t // 2
    c = t % 2
    me = y * 4 + t
    sib = (y, 2 * x + (1 - c))
    xnb = (y, 2 * (1 - x) + c)
    xno = (y, 2 * (1 - x) + (1 - c))
    ynb = (1 - y, t)
    diag = (1 - y, 2 * (1 - x) + c)
    flip = 1 - 2 * c
    near = (4 * y + 2 * (1 - x) + c, 4 * (1 - y) + t, 4 * (1 - y) + 2 * (1 - x) + c)

    def rdma(src, dst, ssem, rsem, dev):
        return pltpu.make_async_remote_copy(
            src_ref=src, dst_ref=dst, send_sem=ssem, recv_sem=rsem,
            device_id=dev, device_id_type=pl.DeviceIdType.MESH)

    cp_wf = pltpu.make_async_copy(wf_hbm, wfv, loc_sem.at[0])
    cp_r = pltpu.make_async_copy(right_hbm.at[:, pl.ds(32 * t, 32), :], rw.at[pl.ds(0, 16)], loc_sem.at[1])
    cp_l = pltpu.make_async_copy(left_hbm, lw.at[pl.ds(0, 16)], loc_sem.at[2])
    cp_wf.start()
    cp_r.start()
    cp_l.start()

    barrier = pltpu.get_barrier_semaphore()
    for q in range(1, 8):
        d = (me + q) % 8
        pl.semaphore_signal(barrier, inc=1, device_id=(d // 4, d % 4), device_id_type=pl.DeviceIdType.MESH)
    pl.semaphore_wait(barrier, 7)

    def l_sib():
        return rdma(left_hbm, lw.at[pl.ds(16, 16)], l_ssem.at[0], l_rsem.at[0], sib)

    def l_dir(i):
        return rdma(left_hbm.at[pl.ds(8 * y + 2 * i, 2)], lw.at[pl.ds(32 + 2 * i, 2)],
                    l_ssem.at[1 + i], l_rsem.at[1 + i], xnb)

    def l_step(i, kind):
        src, dst, dev = ((32, 40, sib), (32, 48, ynb), (48, 56, sib))[kind]
        return rdma(lw.at[pl.ds(src + 2 * i, 2)], lw.at[pl.ds(dst + 2 * i, 2)],
                    lx_ssem.at[kind, i], lx_rsem.at[kind, i], dev)

    def r_send(i):
        first, rows, dst, dev = (
            (0, 2 * x + (1 - c), 16, sib),
            (8 * y, 2 * (1 - x) + c, 32, xnb),
            (8 * y, 2 * (1 - x) + (1 - c), 40, xno),
            (8 * (1 - y), 2 * (1 - x) + c, 48, xnb),
            (8 * (1 - y), 2 * (1 - x) + (1 - c), 56, xno),
        )[i]
        n = 16 if i == 0 else 8
        return rdma(right_hbm.at[pl.ds(first, n), pl.ds(32 * rows, 32), :], rw.at[pl.ds(dst, n)],
                    r_ssem.at[i], r_rsem.at[i], dev)

    for i in range(4):
        l_dir(i).start()
    for i in range(5):
        r_send(i).start()
    l_sib().start()

    row16 = lax.broadcasted_iota(jnp.int32, (PAIR, BOND), 0)
    lane16 = lax.broadcasted_iota(jnp.int32, (PAIR, BOND), 1)
    packed = jnp.zeros((PAIR, BOND), F32)
    for k in range(16):
        place = (lane16 == row16 + 16 * k).astype(F32).astype(BF16)
        packed = packed + jnp.dot(two_ref[k], place, preferred_element_type=F32)
    wt[0] = packed.astype(BF16)

    def w_send(i):
        return rdma(wt.at[0], wt.at[1 + i], w_ssem.at[i], w_rsem.at[i], (sib, xnb, xno)[i])

    for i in range(3):
        w_send(i).start()

    rr = lax.broadcasted_iota(jnp.int32, (BOND, BOND), 0) % 16
    cc = lax.broadcasted_iota(jnp.int32, (BOND, BOND), 1) % 16
    mask[...] = (rr == cc).astype(F32)

    cp_wf.wait()

    def sumsq(i, s):
        blk = wfv[pl.ds(pl.multiple_of(i * 256, 256), 256), :]
        return s + jnp.sum((blk * blk).reshape(32, 8, 128), axis=0)

    total = lax.fori_loop(0, 32, sumsq, jnp.zeros((8, 128), F32))
    total = jnp.sum(jnp.sum(total, axis=1, keepdims=True), axis=0, keepdims=True)
    scale = jnp.broadcast_to(jnp.sqrt(total * (1.0 / ELEMS)), (1, 128))

    wfo = wfv.at[pl.ds(pl.multiple_of(2048 * t, 2048), 2048), :]
    own = pl.ds(pl.multiple_of(32 * t, 32), 32)
    for p in range(PAIR):
        for h in range(2):
            for bt in range(2):
                first = 4096 * h + (p // 4) * 8 + bt * 4 + p % 4
                blk = (wfv[pl.ds(first, 128, stride=32), :] / scale).T
                tmp[bt] = blk
                uT[h, p, pl.ds(128 * bt, 128), :] = blk.astype(BF16)
            vb[0, p, :, pl.ds(128 * h, 128)] = tmp[y, own, :]
        first = (p // 4) * 8 + p % 4
        lo = wfo[pl.ds(first, 64, stride=32), :]
        hi = wfo[pl.ds(first + 4, 64, stride=32), :]
        osb[p] = jnp.where(y == 0, lo, hi) / scale
    vb[2] = jnp.zeros((PAIR, COLS, BOND), F32)
    betas[...] = jnp.zeros((1, 128), F32)

    def out_copy(j):
        return pltpu.make_async_copy(osb, kry_hbm.at[j], o_sem.at[0])

    out_copy(0).start()

    def u_part(h, m, dev):
        return uT.at[h, pl.ds(4 * m, 4), pl.ds(pl.multiple_of(32 * dev, 32), 32), :]

    def u_own(h, m, s):
        part = u_part(h, m, me)
        return rdma(part, part, u_ssem.at[h, m, s], u_rsem.at[h, m, s], (xnb, ynb, diag, sib)[s])

    def u_got(h, m, s):
        part = u_part(h, m, (near + (me + flip,))[s])
        return rdma(part, part, u_ssem.at[h, m, s], u_rsem.at[h, m, s], (xnb, ynb, diag, sib)[s])

    def u_relay(h, m, s):
        part = u_part(h, m, near[s])
        return rdma(part, part, f_ssem.at[h, m, s], f_rsem.at[h, m, s], sib)

    def u_relayed(h, m, s):
        part = u_part(h, m, near[s] + flip)
        return rdma(part, part, f_ssem.at[h, m, s], f_rsem.at[h, m, s], sib)

    def relay_all(h, m):
        for s in range(3):
            u_got(h, m, s).wait_recv()
            u_relay(h, m, s).start()

    def r_stage(h, k0, nk, n):
        lhs = rw[pl.ds(k0, nk)].reshape(nk * COLS, BOND)
        rhs = jnp.concatenate([uT[h, 2 * n], uT[h, 2 * n + 1]], axis=1)
        res = jnp.dot(lhs, rhs, preferred_element_type=F32).astype(BF16)
        yb[pl.ds(k0, nk), 2 * n] = res[:, :HALF].reshape(nk, COLS, HALF)
        yb[pl.ds(k0, nk), 2 * n + 1] = res[:, HALF:].reshape(nk, COLS, HALF)

    def wl_stage(h, s):
        k0 = s * BLOCK
        for k in range(BLOCK):
            rhs = jnp.concatenate(
                [yb[k0 + k, :, pl.ds(16 * i, 16), :].reshape(BOND, HALF) for i in range(2)], axis=1)
            res = jnp.dot(bd[k0 + k], rhs, preferred_element_type=F32).astype(BF16)
            for i in range(2):
                zb[:, pl.ds(16 * i, 16), pl.ds(HALF * k, HALF)] = (
                    res[:, HALF * i:HALF * (i + 1)].reshape(PAIR, 16, HALF))
        lhs = zb[...].reshape(PAIR * COLS, BLOCK * HALF)
        rhs = lw[pl.ds(k0, BLOCK), pl.ds(pl.multiple_of(HALF * h, HALF), HALF), :].reshape(BLOCK * HALF, BOND)
        res = jnp.dot(lhs, rhs, preferred_element_type=F32)
        acc[...] = acc[...] + res.reshape(PAIR, COLS, BOND)

    def build_bd(g):
        slot = (g // 4) * 2 + (1 - g // 4) * (g // 2) + (g // 4) * (g % 2)
        part = (1 - g // 4) * (g % 2) + (g // 4) * ((y + (g - 4 * (g // 4)) // 2) % 2)
        lanes = pl.multiple_of(128 * part, 128)
        ops = wt[slot, :, pl.ds(lanes, 128)].astype(F32).T.astype(BF16)
        e_t = (lax.broadcasted_iota(jnp.int32, (PAIR, BOND), 1) // 16
               == lax.broadcasted_iota(jnp.int32, (PAIR, BOND), 0)).astype(F32).astype(BF16)
        e = (lax.broadcasted_iota(jnp.int32, (BOND, PAIR), 0) // 16
             == lax.broadcasted_iota(jnp.int32, (BOND, PAIR), 1)).astype(F32).astype(BF16)
        wide = jnp.dot(ops, e_t, preferred_element_type=F32).astype(BF16)
        for k in range(8):
            full = jnp.dot(e, wide[16 * k:16 * (k + 1), :], preferred_element_type=F32)
            bd[g * 8 + k] = (full * mask[...]).astype(BF16)

    def bd_group(i, s):
        build_bd(2 * s + i)
        return s

    def first_block(s, carry):
        @pl.when(s == 0)
        def _():
            cp_r.wait()
            cp_l.wait()

        @pl.when(s == 1)
        def _():
            w_send(0).wait_recv()
            r_send(0).wait_recv()
            l_sib().wait_recv()

        @pl.when(s == 2)
        def _():
            w_send(1).wait_recv()
            w_send(2).wait_recv()

        lax.fori_loop(0, 2, bd_group, s)

        @pl.when(s < 2)
        def _():
            l_dir(s).wait_recv()
            l_step(s, 0).start()
            l_step(s, 1).start()

        @pl.when(s == 2)
        def _():
            for i in range(2, 4):
                l_dir(i).wait_recv()
                l_step(i, 0).start()
                l_step(i, 1).start()
            r_send(1).wait_recv()
            r_send(2).wait_recv()
            for i in range(4):
                l_step(i, 0).wait_recv()

        @pl.when(s == 3)
        def _():
            for i in range(4):
                l_step(i, 1).wait_recv()
                l_step(i, 2).start()
            r_send(3).wait_recv()
            r_send(4).wait_recv()
            for i in range(4):
                l_step(i, 2).wait_recv()

        def half(h, carry):
            for n in range(8):
                r_stage(h, s * BLOCK, BLOCK, n)
            wl_stage(h, s)
            return carry

        lax.fori_loop(0, 2, half, 0)
        return carry

    def gather_r(i, carry):
        @pl.when(i < 4)
        def _():
            relay_all(0, i)

        @pl.when(i >= 1)
        def _():
            later_r(0, i - 1)

        return carry

    def later_r(h, m):
        u_got(h, m, 3).wait_recv()
        for s in range(3):
            u_relayed(h, m, s).wait_recv()
        for n in range(2):
            r_stage(h, 0, TERMS, 2 * m + n)

    def gather_wl(s, carry):
        relay_all(1, s)
        wl_stage(0, s)
        return carry

    def second_r(m, carry):
        later_r(1, m)
        for h in range(2):
            for s in range(4):
                u_own(h, m, s).wait_send()
            for s in range(3):
                u_relay(h, m, s).wait_send()
        return carry

    def second_wl(s, carry):
        wl_stage(1, s)
        return carry

    def x_copy(par, q):
        dest = (t + q) % 4
        return rdma(xs.at[dest], xr.at[par, t], x_ssem.at[q - 1], x_rsem.at[par, q - 1], (y, dest))

    def x_recv(par, q):
        rdma(xs.at[0], xr.at[par, (t + 4 - q) % 4], x_ssem.at[q - 1], x_rsem.at[par, q - 1], sib).wait_recv()

    def put_out(vec, par):
        for d in range(2):
            for i in range(4):
                blk = jnp.concatenate(
                    [vb[vec, 4 * i + k, :, pl.ds(128 * d, 128)] for k in range(4)], axis=0).T
                xs[2 * d, i] = blk[:64]
                xs[2 * d + 1, i] = blk[64:]
        xr[par, t] = xs[t]

    def x_start(par):
        for q in range(1, 4):
            x_copy(par, q).start()

    def x_wait_send(par):
        for q in range(1, 4):
            x_copy(par, q).wait_send()

    def merge_out(j, par):
        for q in range(1, 4):
            x_recv(par, q)
        out_copy(0).wait()
        seg = lax.broadcasted_iota(jnp.int32, (64, 128), 1) // 32
        for i in range(4):
            parts = [xr[par, src, i] for src in range(4)]
            for k in range(4):
                res = parts[k]
                for src in range(4):
                    if src != k:
                        res = jnp.where(seg == src, pltpu.roll(parts[src], (32 * (src - k)) % 128, 1), res)
                osb[4 * i + k] = res
        out_copy(j).start()

    def everywhere(s):
        s = jnp.sum(jnp.sum(s, axis=1, keepdims=True), axis=0, keepdims=True)
        return jnp.broadcast_to(s, (1, 128))

    def fold(v):
        v = v[:, :HALF] + v[:, HALF:]
        return jnp.sum(v.reshape(COLS // 8, 8, 128), axis=0)

    def wide(row):
        return jnp.concatenate([row, row], axis=1)

    def step(j, carry):
        acc[...] = jnp.zeros((PAIR, COLS, BOND), F32)

        @pl.when(j == 0)
        def _():
            lax.fori_loop(0, 4, first_block, 0)

        @pl.when(j > 0)
        def _():
            lax.fori_loop(0, 5, gather_r, 0)
            lax.fori_loop(0, 4, gather_wl, 0)
            x_start((j + 1) % 2)
            lax.fori_loop(0, 4, second_r, 0)
            lax.fori_loop(0, 4, second_wl, 0)

        cur = j % 3
        prev = (j + 2) % 3
        nxt = (j + 1) % 3
        par = j % 2
        beta_prev = wide(betas[...])
        zero = jnp.zeros((8, 128), F32)

        def pass1(p, s):
            a_s, t_s, v_s = s
            w = acc[p]
            v = vb[cur, p]
            r = w - beta_prev * vb[prev, p]
            vb[nxt, p] = r
            return a_s + fold(w * v), t_s + fold(r * v), v_s + fold(v * v)

        a_s, t_s, v_s = lax.fori_loop(0, PAIR, pass1, (zero, zero, zero))
        a_d, t_d, v_d = everywhere(a_s), everywhere(t_s), everywhere(v_s)
        shift = jnp.where(v_d > 0.0, t_d / jnp.where(v_d > 0.0, v_d, 1.0), 0.0)
        shift_w = wide(shift)

        def pass2(p, s):
            q_s, p_s = s
            v = vb[cur, p]
            r = vb[nxt, p] - shift_w * v
            vb[nxt, p] = r
            return q_s + fold(r * r), p_s + fold(r * v)

        q_s, p_s = lax.fori_loop(0, PAIR, pass2, (zero, zero))
        st[par, me] = jnp.concatenate(
            [a_d, shift, v_d, everywhere(q_s), everywhere(p_s), jnp.zeros((3, 128), F32)], axis=0)

        def st_copy(q):
            d = (me + q) % 8
            return rdma(st.at[par, me], st.at[par, me], st_ssem.at[q - 1], st_rsem.at[q - 1], (d // 4, d % 4))

        for q in range(1, 8):
            st_copy(q).start()
        for q in range(1, 8):
            src = (me + 8 - q) % 8
            rdma(st.at[par, me], st.at[par, src], st_ssem.at[q - 1], st_rsem.at[q - 1], sib).wait_recv()

        alpha = st[par, 0][0:1]
        for d in range(1, 8):
            alpha = alpha + st[par, d][0:1]
        alpha = alpha * (1.0 / ELEMS)
        beta2 = jnp.zeros((1, 128), F32)
        for d in range(8):
            tile = st[par, d]
            gap = alpha - tile[1:2]
            beta2 = beta2 + (tile[3:4] - 2.0 * gap * tile[4:5] + gap * gap * tile[2:3])
        beta = jnp.sqrt(beta2 * (1.0 / ELEMS))
        betas[...] = beta
        ab_ref[j] = jnp.concatenate([alpha, beta, jnp.zeros((6, 128), F32)], axis=0)
        gap_w = wide(alpha - shift)
        beta_w = wide(beta)
        rows = pl.ds(pl.multiple_of(32 * me, 32), 32)

        def pass3(m, carry):
            for i in range(4):
                p = 4 * m + i
                v = (vb[nxt, p] - gap_w * vb[cur, p]) / beta_w
                vb[nxt, p] = v
                uT[0, p, rows, :] = v[:, :HALF].astype(BF16)
                uT[1, p, rows, :] = v[:, HALF:].astype(BF16)

            @pl.when(j < STEPS - 1)
            def _():
                for s in range(4):
                    u_own(0, m, s).start()

            return carry

        lax.fori_loop(0, 4, pass3, 0)

        @pl.when(j < STEPS - 1)
        def _():
            for m in range(4):
                for s in range(4):
                    u_own(1, m, s).start()

        @pl.when(j > 0)
        def _():
            x_wait_send(1 - par)

        put_out(nxt, par)

        @pl.when(j > 0)
        def _():
            merge_out(j, 1 - par)

        for q in range(1, 8):
            st_copy(q).wait_send()
        return carry

    lax.fori_loop(0, STEPS, step, 0)

    last = (STEPS - 1) % 2
    x_start(last)
    x_wait_send(last)
    merge_out(STEPS, last)
    out_copy(0).wait()

    l_sib().wait_send()
    for i in range(3):
        w_send(i).wait_send()
    for i in range(5):
        r_send(i).wait_send()
    for i in range(4):
        l_dir(i).wait_send()
        for kind in range(3):
            l_step(i, kind).wait_send()


def solution(mesh):
    def body_fn(wavefunc, left_loc, two_loc, right_loc):
        bond, phys = wavefunc.shape[0], wavefunc.shape[1]
        wf = wavefunc.reshape(bond, phys, phys, 2, 128).transpose(0, 1, 3, 2, 4).reshape(-1, 128)
        dma = pltpu.SemaphoreType.DMA
        kry, ab = pl.pallas_call(
            lanczos_kernel,
            out_shape=(
                jax.ShapeDtypeStruct((STEPS + 1, PAIR, 64, 128), F32),
                jax.ShapeDtypeStruct((STEPS, 8, 128), F32),
            ),
            in_specs=[
                pl.BlockSpec(memory_space=pl.ANY),
                pl.BlockSpec(memory_space=pl.ANY),
                pl.BlockSpec(memory_space=pltpu.VMEM),
                pl.BlockSpec(memory_space=pl.ANY),
            ],
            out_specs=(pl.BlockSpec(memory_space=pl.ANY), pl.BlockSpec(memory_space=pltpu.VMEM)),
            scratch_shapes=[
                pltpu.VMEM((8192, 128), F32),
                pltpu.VMEM((TERMS, COLS, BOND), BF16),
                pltpu.VMEM((TERMS, BOND, BOND), BF16),
                pltpu.VMEM((TERMS, BOND, BOND), BF16),
                pltpu.VMEM((4, PAIR, BOND), BF16),
                pltpu.VMEM((BOND, BOND), F32),
                pltpu.VMEM((TERMS, PAIR, COLS, HALF), BF16),
                pltpu.VMEM((PAIR, COLS, BLOCK * HALF), BF16),
                pltpu.VMEM((2, PAIR, BOND, HALF), BF16),
                pltpu.VMEM((PAIR, COLS, BOND), F32),
                pltpu.VMEM((3, PAIR, COLS, BOND), F32),
                pltpu.VMEM((2, 128, 128), F32),
                pltpu.VMEM((2, 8, 8, 128), F32),
                pltpu.VMEM((1, 128), F32),
                pltpu.VMEM((4, 4, 64, 128), F32),
                pltpu.VMEM((2, 4, 4, 64, 128), F32),
                pltpu.VMEM((PAIR, 64, 128), F32),
                dma((3,)),
                dma((3,)), dma((3,)),
                dma((5,)), dma((5,)),
                dma((5,)), dma((5,)),
                dma((3, 4)), dma((3, 4)),
                dma((2, 4, 4)), dma((2, 4, 4)),
                dma((2, 4, 3)), dma((2, 4, 3)),
                dma((7,)), dma((7,)),
                dma((3,)), dma((2, 3)),
                dma((1,)),
            ],
            compiler_params=pltpu.CompilerParams(
                collective_id=0, has_side_effects=True, vmem_limit_bytes=66 * 1000 * 1000),
        )(wf, left_loc, two_loc, right_loc)
        krylov = kry.transpose(0, 2, 1, 3).reshape(STEPS + 1, 64, phys, phys, 128)
        return krylov, ab[:, 0, 0], ab[:, 1, 0]

    return jax.shard_map(
        body_fn, mesh=mesh,
        in_specs=(P(), P('terms'), P('terms'), P('terms', 'rows')),
        out_specs=(P(None, 'terms', None, None, 'rows'), P(), P()), check_vma=False)
```

time: 246 us -> 222 us (0.902)
  Pallas kernels: 236 us -> 213 us
    pallas_call x1, Pallas kernels: 236 us -> 213 us  [body_fn(): pl.pallas_call(lanczos_kernel, out_shape=(jax.ShapeDtypeStruct((STEPS + 1...]
where the time goes in v3:
time: 222 us; the launch traced here: 221 us
  Pallas kernels  213 us (96%)
  local copies, waits for them, and re-layouts  7.69 us (3%)
    pallas_call x1, Pallas kernels, body_fn(): pl.pallas_call(lanczos_kernel, out_shape=(jax.ShapeDtypeStruct((STEPS + 1...  213 us
    unnamed x1, local copies, waits for them, and re-layouts  6.24 us

profile of v3, /device:TPU:0, one launch (start us, length us, event | category | flops | bytes accessed | tf_op | source)
XLA Modules:
  0.0 220.9 jit_solution(6746230460725438860)
XLA Ops:
  0.6 212.5 %shard_map.67 = (f32[7,16,64,128]{3,2,1,0:T(8,128)}, f32[6,8,128]{2,1,0:T(8,128)}) custom-call(f32[8192,128]{1,0:T(8,128)} %bitcast.8, bf16[16,256,256]{2,1,0:T(8,128)(2,1)} %left_hbm.1, bf16[16,16,16]{2,1,0:T(8,128)(2,1)} %two_ref.1, bf16[16,128,256]{2,1,0:T(8,128)(2,1)} %right_hbm.1), custom_call_target="tpu_custom_call" | custom-call | tf_op jit(solution)/shard_map/pallas_call | solution.py:474
  213.2 1.5 slice_reduce_fusion
  214.6 6.2 %copy.10 = f32[7,64,4,4,128]{4,3,2,1,0:T(4,128)} copy(f32[7,64,4,4,128]{4,1,3,2,0:T(8,128)} %bitcast.9) | data formatting | bytes 7340032

commit v4 on v3

--- a/solution.py
+++ b/solution.py
@@ -19,7 +19,7 @@
 
 def lanczos_kernel(
     wf_hbm, left_hbm, two_ref, right_hbm, kry_hbm, ab_ref,
-    wfv, rw, lw, bd, wt, mask, yb, zb, uT, acc, vb, tmp, st, betas, xs, xr, osb,
+    wfv, rw, lw, lx, bd, wt, mask, yb, zb, uT, acc, vb, tmp, st, betas, coef, xs, xr, osb,
     loc_sem, w_ssem, w_rsem, r_ssem, r_rsem, l_ssem, l_rsem, lx_ssem, lx_rsem,
     u_ssem, u_rsem, f_ssem, f_rsem, st_ssem, st_rsem, x_ssem, x_rsem, o_sem,
 ):
@@ -57,14 +57,32 @@
     def l_sib():
         return rdma(left_hbm, lw.at[pl.ds(16, 16)], l_ssem.at[0], l_rsem.at[0], sib)
 
-    def l_dir(i):
-        return rdma(left_hbm.at[pl.ds(8 * y + 2 * i, 2)], lw.at[pl.ds(32 + 2 * i, 2)],
-                    l_ssem.at[1 + i], l_rsem.at[1 + i], xnb)
+    def l_dir(i, part):
+        rows = pl.ds(0, 256) if part == 0 else pl.ds(128, 128)
+        return rdma(left_hbm.at[pl.ds(8 * y + 2 * i, 2), rows, pl.ds(128 * part, 128)],
+                    lx.at[pl.ds(2 * i, 2), pl.ds(256 * part, 256 - 128 * part), :],
+                    l_ssem.at[1 + 2 * i + part], l_rsem.at[1 + 2 * i + part], xnb)
 
     def l_step(i, kind):
-        src, dst, dev = ((32, 40, sib), (32, 48, ynb), (48, 56, sib))[kind]
-        return rdma(lw.at[pl.ds(src + 2 * i, 2)], lw.at[pl.ds(dst + 2 * i, 2)],
+        src, dst, dev = ((0, 8, sib), (0, 16, ynb), (16, 24, sib))[kind]
+        return rdma(lx.at[pl.ds(src + 2 * i, 2)], lx.at[pl.ds(dst + 2 * i, 2)],
                     lx_ssem.at[kind, i], lx_rsem.at[kind, i], dev)
+
+    def l_take(i):
+        for part in range(2):
+            l_dir(i, part).wait_recv()
+        l_step(i, 0).start()
+        l_step(i, 1).start()
+
+    def l_unpack(k, s):
+        src = 16 * (s - 2) + k
+        dst = 16 * s + k
+        low = lx[src, pl.ds(128, 128), :]
+        lw[dst, pl.ds(0, 128), pl.ds(0, 128)] = lx[src, pl.ds(0, 128), :]
+        lw[dst, pl.ds(128, 128), pl.ds(0, 128)] = low
+        lw[dst, pl.ds(0, 128), pl.ds(128, 128)] = low.astype(F32).T.astype(BF16)
+        lw[dst, pl.ds(128, 128), pl.ds(128, 128)] = lx[src, pl.ds(256, 128), :]
+        return s
 
     def r_send(i):
         first, rows, dst, dev = (
@@ -79,7 +97,8 @@
                     r_ssem.at[i], r_rsem.at[i], dev)
 
     for i in range(4):
-        l_dir(i).start()
+        for part in range(2):
+            l_dir(i, part).start()
     for i in range(5):
         r_send(i).start()
     l_sib().start()
@@ -125,12 +144,12 @@
         first = (p // 4) * 8 + p % 4
         lo = wfo[pl.ds(first, 64, stride=32), :]
         hi = wfo[pl.ds(first + 4, 64, stride=32), :]
-        osb[p] = jnp.where(y == 0, lo, hi) / scale
+        osb[0, pl.ds(p, 64, stride=16), :] = jnp.where(y == 0, lo, hi) / scale
     vb[2] = jnp.zeros((PAIR, COLS, BOND), F32)
     betas[...] = jnp.zeros((1, 128), F32)
 
     def out_copy(j):
-        return pltpu.make_async_copy(osb, kry_hbm.at[j], o_sem.at[0])
+        return pltpu.make_async_copy(osb.at[j % 2], kry_hbm.at[j], o_sem.at[j % 2])
 
     out_copy(0).start()
 
@@ -218,30 +237,31 @@
 
         @pl.when(s < 2)
         def _():
-            l_dir(s).wait_recv()
-            l_step(s, 0).start()
-            l_step(s, 1).start()
+            for i in range(2):
+                @pl.when(s == i)
+                def _(i=i):
+                    l_take(i)
 
         @pl.when(s == 2)
         def _():
-            for i in range(2, 4):
-                l_dir(i).wait_recv()
-                l_step(i, 0).start()
-                l_step(i, 1).start()
+            l_take(2)
+            l_take(3)
+            for i in range(4):
+                l_step(i, 0).wait_recv()
+            lax.fori_loop(0, 16, l_unpack, s)
             r_send(1).wait_recv()
             r_send(2).wait_recv()
-            for i in range(4):
-                l_step(i, 0).wait_recv()
 
         @pl.when(s == 3)
         def _():
             for i in range(4):
                 l_step(i, 1).wait_recv()
                 l_step(i, 2).start()
+            for i in range(4):
+                l_step(i, 2).wait_recv()
+            lax.fori_loop(0, 16, l_unpack, s)
             r_send(3).wait_recv()
             r_send(4).wait_recv()
-            for i in range(4):
-                l_step(i, 2).wait_recv()
 
         def half(h, carry):
             for n in range(8):
@@ -299,7 +319,7 @@
         for d in range(2):
             for i in range(4):
                 blk = jnp.concatenate(
-                    [vb[vec, 4 * i + k, :, pl.ds(128 * d, 128)] for k in range(4)], axis=0).T
+                    [vec[4 * i + k, :, pl.ds(128 * d, 128)] for k in range(4)], axis=0).T
                 xs[2 * d, i] = blk[:64]
                 xs[2 * d + 1, i] = blk[64:]
         xr[par, t] = xs[t]
@@ -312,10 +332,7 @@
         for q in range(1, 4):
             x_copy(par, q).wait_send()
 
-    def merge_out(j, par):
-        for q in range(1, 4):
-            x_recv(par, q)
-        out_copy(0).wait()
+    def merged(par):
         seg = lax.broadcasted_iota(jnp.int32, (64, 128), 1) // 32
         for i in range(4):
             parts = [xr[par, src, i] for src in range(4)]
@@ -324,7 +341,18 @@
                 for src in range(4):
                     if src != k:
                         res = jnp.where(seg == src, pltpu.roll(parts[src], (32 * (src - k)) % 128, 1), res)
-                osb[4 * i + k] = res
+                yield 4 * i + k, res
+
+    def merge_out(j, par):
+        for q in range(1, 4):
+            x_recv(par, q)
+
+        @pl.when(j > 1)
+        def _():
+            out_copy(j - 2).wait()
+
+        for p, res in merged(par):
+            osb[j % 2, pl.ds(p, 64, stride=16), :] = res
         out_copy(j).start()
 
     def everywhere(s):
@@ -357,6 +385,13 @@
         prev = (j + 2) % 3
         nxt = (j + 1) % 3
         par = j % 2
+
+        @pl.when(j == STEPS - 1)
+        def _():
+            x_wait_send(1 - par)
+            put_out(acc, par)
+            x_start(par)
+
         beta_prev = wide(betas[...])
         zero = jnp.zeros((8, 128), F32)
 
@@ -390,6 +425,11 @@
 
         for q in range(1, 8):
             st_copy(q).start()
+
+        @pl.when(j > 0)
+        def _():
+            merge_out(j, 1 - par)
+
         for q in range(1, 8):
             src = (me + 8 - q) % 8
             rdma(st.at[par, me], st.at[par, src], st_ssem.at[q - 1], st_rsem.at[q - 1], sib).wait_recv()
@@ -405,6 +445,8 @@
             beta2 = beta2 + (tile[3:4] - 2.0 * gap * tile[4:5] + gap * gap * tile[2:3])
         beta = jnp.sqrt(beta2 * (1.0 / ELEMS))
         betas[...] = beta
+        coef[0] = alpha
+        coef[1] = beta_prev[:, :HALF]
         ab_ref[j] = jnp.concatenate([alpha, beta, jnp.zeros((6, 128), F32)], axis=0)
         gap_w = wide(alpha - shift)
         beta_w = wide(beta)
@@ -418,30 +460,24 @@
                 uT[0, p, rows, :] = v[:, :HALF].astype(BF16)
                 uT[1, p, rows, :] = v[:, HALF:].astype(BF16)
 
-            @pl.when(j < STEPS - 1)
-            def _():
-                for s in range(4):
-                    u_own(0, m, s).start()
-
+            for s in range(4):
+                u_own(0, m, s).start()
             return carry
 
-        lax.fori_loop(0, 4, pass3, 0)
-
         @pl.when(j < STEPS - 1)
         def _():
+            lax.fori_loop(0, 4, pass3, 0)
             for m in range(4):
                 for s in range(4):
                     u_own(1, m, s).start()
 
-        @pl.when(j > 0)
+        @pl.when((j > 0) & (j < STEPS - 1))
         def _():
             x_wait_send(1 - par)
 
-        put_out(nxt, par)
-
-        @pl.when(j > 0)
-        def _():
-            merge_out(j, 1 - par)
+        @pl.when(j < STEPS - 1)
+        def _():
+            put_out(vb.at[nxt], par)
 
         for q in range(1, 8):
             st_copy(q).wait_send()
@@ -450,10 +486,17 @@
     lax.fori_loop(0, STEPS, step, 0)
 
     last = (STEPS - 1) % 2
-    x_start(last)
+    for q in range(1, 4):
+        x_recv(last, q)
+    out_copy(STEPS - 2).wait()
+    for p, res in merged(last):
+        at = pl.ds(p, 64, stride=16)
+        res = res - coef[0] * osb[(STEPS - 1) % 2, at, :] - coef[1] * osb[STEPS % 2, at, :]
+        osb[STEPS % 2, at, :] = res / betas[...]
+    out_copy(STEPS).start()
     x_wait_send(last)
-    merge_out(STEPS, last)
-    out_copy(0).wait()
+    out_copy(STEPS - 1).wait()
+    out_copy(STEPS).wait()
 
     l_sib().wait_send()
     for i in range(3):
@@ -461,7 +504,8 @@
     for i in range(5):
         r_send(i).wait_send()
     for i in range(4):
-        l_dir(i).wait_send()
+        for part in range(2):
+            l_dir(i, part).wait_send()
         for kind in range(3):
             l_step(i, kind).wait_send()
 
@@ -474,7 +518,7 @@
         kry, ab = pl.pallas_call(
             lanczos_kernel,
             out_shape=(
-                jax.ShapeDtypeStruct((STEPS + 1, PAIR, 64, 128), F32),
+                jax.ShapeDtypeStruct((STEPS + 1, 64 * PAIR, 128), F32),
                 jax.ShapeDtypeStruct((STEPS, 8, 128), F32),
             ),
             in_specs=[
@@ -488,6 +532,7 @@
                 pltpu.VMEM((8192, 128), F32),
                 pltpu.VMEM((TERMS, COLS, BOND), BF16),
                 pltpu.VMEM((TERMS, BOND, BOND), BF16),
+                pltpu.VMEM((32, 384, 128), BF16),
                 pltpu.VMEM((TERMS, BOND, BOND), BF16),
                 pltpu.VMEM((4, PAIR, BOND), BF16),
                 pltpu.VMEM((BOND, BOND), F32),
@@ -499,24 +544,25 @@
                 pltpu.VMEM((2, 128, 128), F32),
                 pltpu.VMEM((2, 8, 8, 128), F32),
                 pltpu.VMEM((1, 128), F32),
+                pltpu.VMEM((2, 1, 128), F32),
                 pltpu.VMEM((4, 4, 64, 128), F32),
                 pltpu.VMEM((2, 4, 4, 64, 128), F32),
-                pltpu.VMEM((PAIR, 64, 128), F32),
+                pltpu.VMEM((2, 64 * PAIR, 128), F32),
                 dma((3,)),
                 dma((3,)), dma((3,)),
                 dma((5,)), dma((5,)),
-                dma((5,)), dma((5,)),
+                dma((9,)), dma((9,)),
                 dma((3, 4)), dma((3, 4)),
                 dma((2, 4, 4)), dma((2, 4, 4)),
                 dma((2, 4, 3)), dma((2, 4, 3)),
                 dma((7,)), dma((7,)),
                 dma((3,)), dma((2, 3)),
-                dma((1,)),
+                dma((2,)),
             ],
             compiler_params=pltpu.CompilerParams(
                 collective_id=0, has_side_effects=True, vmem_limit_bytes=66 * 1000 * 1000),
         )(wf, left_loc, two_loc, right_loc)
-        krylov = kry.transpose(0, 2, 1, 3).reshape(STEPS + 1, 64, phys, phys, 128)
+        krylov = kry.reshape(STEPS + 1, 64, phys, phys, 128)
         return krylov, ab[:, 0, 0], ab[:, 1, 0]
 
     return jax.shard_map(

time: 222 us -> 212 us (0.955)
  Pallas kernels: 213 us -> 205 us
    pallas_call x1, Pallas kernels: 213 us -> 205 us  [body_fn(): pl.pallas_call(lanczos_kernel, out_shape=(jax.ShapeDtypeStruct((STEPS + 1...]
where the time goes in v4:
time: 212 us; the launch traced here: 211 us
  Pallas kernels  205 us (97%)
  local copies, waits for them, and re-layouts  5.96 us (3%)
    pallas_call x1, Pallas kernels, body_fn(): pl.pallas_call(lanczos_kernel, out_shape=(jax.ShapeDtypeStruct((STEPS + 1...  205 us
    unnamed x1, local copies, waits for them, and re-layouts  4.5 us

profile of v4, /device:TPU:0, one launch (start us, length us, event | category | flops | bytes accessed | tf_op | source)
XLA Modules:
  0.0 211.3 jit_solution(4262821441767639536)
XLA Ops:
  0.6 204.7 %shard_map.67 = (f32[7,1024,128]{2,1,0:T(8,128)}, f32[6,8,128]{2,1,0:T(8,128)}) custom-call(f32[8192,128]{1,0:T(8,128)} %bitcast.6, bf16[16,256,256]{2,1,0:T(8,128)(2,1)} %left_hbm.1, bf16[16,16,16]{2,1,0:T(8,128)(2,1)} %two_ref.1, bf16[16,128,256]{2,1,0:T(8,128)(2,1)} %right_hbm.1), custom_call_target="tpu_custom_call" | custom-call | tf_op jit(solution)/shard_map/pallas_call | solution.py:518
  205.4 1.5 slice_reduce_fusion
  206.8 4.5 %copy.10 = f32[7,64,4,4,128]{4,3,2,1,0:T(4,128)} copy(f32[7,64,4,4,128]{4,3,2,1,0:T(4,128)} %bitcast.7) | data formatting | bytes 7340032

commit v5 on v4

--- a/solution.py
+++ b/solution.py
@@ -276,6 +276,8 @@
         @pl.when(i < 4)
         def _():
             relay_all(0, i)
+            for s in range(4):
+                u_own(1, i, s).start()
 
         @pl.when(i >= 1)
         def _():
@@ -467,9 +469,6 @@
         @pl.when(j < STEPS - 1)
         def _():
             lax.fori_loop(0, 4, pass3, 0)
-            for m in range(4):
-                for s in range(4):
-                    u_own(1, m, s).start()
 
         @pl.when((j > 0) & (j < STEPS - 1))
         def _():

time: 212 us -> 212 us (level)
  no operation moved by 1% of the time
where the time goes in v5:
time: 212 us; the launch traced here: 211 us
  Pallas kernels  205 us (97%)
  local copies, waits for them, and re-layouts  5.96 us (3%)
    pallas_call x1, Pallas kernels, body_fn(): pl.pallas_call(lanczos_kernel, out_shape=(jax.ShapeDtypeStruct((STEPS + 1...  205 us
    unnamed x1, local copies, waits for them, and re-layouts  4.5 us

profile of v5, /device:TPU:0, one launch (start us, length us, event | category | flops | bytes accessed | tf_op | source)
XLA Modules:
  0.0 211.4 jit_solution(2767924227644941126)
XLA Ops:
  0.6 204.8 %shard_map.67 = (f32[7,1024,128]{2,1,0:T(8,128)}, f32[6,8,128]{2,1,0:T(8,128)}) custom-call(f32[8192,128]{1,0:T(8,128)} %bitcast.6, bf16[16,256,256]{2,1,0:T(8,128)(2,1)} %left_hbm.1, bf16[16,16,16]{2,1,0:T(8,128)(2,1)} %two_ref.1, bf16[16,128,256]{2,1,0:T(8,128)(2,1)} %right_hbm.1), custom_call_target="tpu_custom_call" | custom-call | tf_op jit(solution)/shard_map/pallas_call | solution.py:517
  205.4 1.5 slice_reduce_fusion
  206.9 4.5 %copy.10 = f32[7,64,4,4,128]{4,3,2,1,0:T(4,128)} copy(f32[7,64,4,4,128]{4,3,2,1,0:T(4,128)} %bitcast.7) | data formatting | bytes 7340032

commit v6 on v4

--- a/solution.py
+++ b/solution.py
@@ -74,15 +74,15 @@
         l_step(i, 0).start()
         l_step(i, 1).start()
 
-    def l_unpack(k, s):
-        src = 16 * (s - 2) + k
-        dst = 16 * s + k
+    def l_unpack(k, g):
+        src = 8 * (g - 4) + k
+        dst = 8 * g + k
         low = lx[src, pl.ds(128, 128), :]
         lw[dst, pl.ds(0, 128), pl.ds(0, 128)] = lx[src, pl.ds(0, 128), :]
         lw[dst, pl.ds(128, 128), pl.ds(0, 128)] = low
         lw[dst, pl.ds(0, 128), pl.ds(128, 128)] = low.astype(F32).T.astype(BF16)
         lw[dst, pl.ds(128, 128), pl.ds(128, 128)] = lx[src, pl.ds(256, 128), :]
-        return s
+        return g
 
     def r_send(i):
         first, rows, dst, dev = (
@@ -177,24 +177,23 @@
             u_got(h, m, s).wait_recv()
             u_relay(h, m, s).start()
 
-    def r_stage(h, k0, nk, n):
+    def r_stage(h, k0, nk, m):
         lhs = rw[pl.ds(k0, nk)].reshape(nk * COLS, BOND)
-        rhs = jnp.concatenate([uT[h, 2 * n], uT[h, 2 * n + 1]], axis=1)
+        rhs = jnp.concatenate([uT[h, 4 * m + i] for i in range(4)], axis=1)
         res = jnp.dot(lhs, rhs, preferred_element_type=F32).astype(BF16)
-        yb[pl.ds(k0, nk), 2 * n] = res[:, :HALF].reshape(nk, COLS, HALF)
-        yb[pl.ds(k0, nk), 2 * n + 1] = res[:, HALF:].reshape(nk, COLS, HALF)
-
-    def wl_stage(h, s):
-        k0 = s * BLOCK
-        for k in range(BLOCK):
+        for i in range(4):
+            yb[pl.ds(k0, nk), 4 * m + i] = res[:, HALF * i:HALF * (i + 1)].reshape(nk, COLS, HALF)
+
+    def wl_stage(h, k0, nk, buf=0):
+        for k in range(nk):
             rhs = jnp.concatenate(
                 [yb[k0 + k, :, pl.ds(16 * i, 16), :].reshape(BOND, HALF) for i in range(2)], axis=1)
             res = jnp.dot(bd[k0 + k], rhs, preferred_element_type=F32).astype(BF16)
             for i in range(2):
-                zb[:, pl.ds(16 * i, 16), pl.ds(HALF * k, HALF)] = (
+                zb[buf, :, pl.ds(16 * i, 16), pl.ds(HALF * k, HALF)] = (
                     res[:, HALF * i:HALF * (i + 1)].reshape(PAIR, 16, HALF))
-        lhs = zb[...].reshape(PAIR * COLS, BLOCK * HALF)
-        rhs = lw[pl.ds(k0, BLOCK), pl.ds(pl.multiple_of(HALF * h, HALF), HALF), :].reshape(BLOCK * HALF, BOND)
+        lhs = zb[buf, :, :, pl.ds(0, nk * HALF)].reshape(PAIR * COLS, nk * HALF)
+        rhs = lw[pl.ds(k0, nk), pl.ds(pl.multiple_of(HALF * h, HALF), HALF), :].reshape(nk * HALF, BOND)
         res = jnp.dot(lhs, rhs, preferred_element_type=F32)
         acc[...] = acc[...] + res.reshape(PAIR, COLS, BOND)
 
@@ -212,61 +211,68 @@
             full = jnp.dot(e, wide[16 * k:16 * (k + 1), :], preferred_element_type=F32)
             bd[g * 8 + k] = (full * mask[...]).astype(BF16)
 
-    def bd_group(i, s):
-        build_bd(2 * s + i)
-        return s
+    def first_half(h, k0, nk):
+        for m in range(4):
+            r_stage(h, k0, nk, m)
+        wl_stage(h, k0, nk)
+
+    def bd_group(g, carry):
+        build_bd(g)
+        return carry
 
     def first_block(s, carry):
         @pl.when(s == 0)
         def _():
             cp_r.wait()
             cp_l.wait()
+            lax.fori_loop(0, 2, bd_group, 0)
+            l_take(0)
 
         @pl.when(s == 1)
         def _():
-            w_send(0).wait_recv()
+            for i in range(3):
+                w_send(i).wait_recv()
+            lax.fori_loop(2, 8, bd_group, 0)
+            l_take(1)
             r_send(0).wait_recv()
             l_sib().wait_recv()
 
         @pl.when(s == 2)
         def _():
-            w_send(1).wait_recv()
-            w_send(2).wait_recv()
-
-        lax.fori_loop(0, 2, bd_group, s)
-
-        @pl.when(s < 2)
-        def _():
-            for i in range(2):
-                @pl.when(s == i)
-                def _(i=i):
-                    l_take(i)
-
-        @pl.when(s == 2)
-        def _():
             l_take(2)
             l_take(3)
+            lax.fori_loop(0, 8, l_unpack, 4)
             for i in range(4):
                 l_step(i, 0).wait_recv()
-            lax.fori_loop(0, 16, l_unpack, s)
-            r_send(1).wait_recv()
-            r_send(2).wait_recv()
-
-        @pl.when(s == 3)
-        def _():
+            lax.fori_loop(0, 8, l_unpack, 5)
             for i in range(4):
                 l_step(i, 1).wait_recv()
                 l_step(i, 2).start()
+            r_send(1).wait_recv()
+            r_send(2).wait_recv()
+
+        def half(h, carry):
+            first_half(h, s * BLOCK, BLOCK)
+            return carry
+
+        lax.fori_loop(0, 2, half, 0)
+        return carry
+
+    def last_group(g, carry):
+        @pl.when(g == 6)
+        def _():
+            lax.fori_loop(0, 8, l_unpack, 6)
             for i in range(4):
                 l_step(i, 2).wait_recv()
-            lax.fori_loop(0, 16, l_unpack, s)
+            lax.fori_loop(0, 8, l_unpack, 7)
             r_send(3).wait_recv()
+
+        @pl.when(g == 7)
+        def _():
             r_send(4).wait_recv()
 
         def half(h, carry):
-            for n in range(8):
-                r_stage(h, s * BLOCK, BLOCK, n)
-            wl_stage(h, s)
+            first_half(h, g * 8, 8)
             return carry
 
         lax.fori_loop(0, 2, half, 0)
@@ -283,29 +289,34 @@
 
         return carry
 
-    def later_r(h, m):
+    def u_all(h, m):
         u_got(h, m, 3).wait_recv()
         for s in range(3):
             u_relayed(h, m, s).wait_recv()
-        for n in range(2):
-            r_stage(h, 0, TERMS, 2 * m + n)
+
+    def later_r(h, m):
+        u_all(h, m)
+        r_stage(h, 0, TERMS, m)
 
     def gather_wl(s, carry):
         relay_all(1, s)
-        wl_stage(0, s)
-        return carry
-
-    def second_r(m, carry):
-        later_r(1, m)
+        wl_stage(0, s * BLOCK, BLOCK)
+        return carry
+
+    def second():
+        for m in range(4):
+            u_all(1, m)
+        for m in range(4):
+            r_stage(1, 0, TERMS, m)
+        for s in range(4):
+            wl_stage(1, s * BLOCK, BLOCK, s % 2)
+
+    def sent(m, carry):
         for h in range(2):
             for s in range(4):
                 u_own(h, m, s).wait_send()
             for s in range(3):
                 u_relay(h, m, s).wait_send()
-        return carry
-
-    def second_wl(s, carry):
-        wl_stage(1, s)
         return carry
 
     def x_copy(par, q):
@@ -371,15 +382,16 @@
 
         @pl.when(j == 0)
         def _():
-            lax.fori_loop(0, 4, first_block, 0)
+            lax.fori_loop(0, 3, first_block, 0)
+            lax.fori_loop(6, 8, last_group, 0)
 
         @pl.when(j > 0)
         def _():
             lax.fori_loop(0, 5, gather_r, 0)
             lax.fori_loop(0, 4, gather_wl, 0)
             x_start((j + 1) % 2)
-            lax.fori_loop(0, 4, second_r, 0)
-            lax.fori_loop(0, 4, second_wl, 0)
+            second()
+            lax.fori_loop(0, 4, sent, 0)
 
         cur = j % 3
         prev = (j + 2) % 3
@@ -460,7 +472,7 @@
                 uT[0, p, rows, :] = v[:, :HALF].astype(BF16)
                 uT[1, p, rows, :] = v[:, HALF:].astype(BF16)
 
-            for s in range(4):
+            for s in (2, 0, 1, 3):
                 u_own(0, m, s).start()
             return carry
 
@@ -468,7 +480,7 @@
         def _():
             lax.fori_loop(0, 4, pass3, 0)
             for m in range(4):
-                for s in range(4):
+                for s in (2, 0, 1, 3):
                     u_own(1, m, s).start()
 
         @pl.when((j > 0) & (j < STEPS - 1))
@@ -537,7 +549,7 @@
                 pltpu.VMEM((4, PAIR, BOND), BF16),
                 pltpu.VMEM((BOND, BOND), F32),
                 pltpu.VMEM((TERMS, PAIR, COLS, HALF), BF16),
-                pltpu.VMEM((PAIR, COLS, BLOCK * HALF), BF16),
+                pltpu.VMEM((2, PAIR, COLS, BLOCK * HALF), BF16),
                 pltpu.VMEM((2, PAIR, BOND, HALF), BF16),
                 pltpu.VMEM((PAIR, COLS, BOND), F32),
                 pltpu.VMEM((3, PAIR, COLS, BOND), F32),

time: 212 us -> 219 us (1.033)
  Pallas kernels: 205 us -> 212 us
    pallas_call x1, Pallas kernels: 205 us -> 212 us  [body_fn(): pl.pallas_call(lanczos_kernel, out_shape=(jax.ShapeDtypeStruct((STEPS + 1...]
where the time goes in v6:
time: 219 us; the launch traced here: 218 us
  Pallas kernels  212 us (97%)
  local copies, waits for them, and re-layouts  5.96 us (3%)
    pallas_call x1, Pallas kernels, body_fn(): pl.pallas_call(lanczos_kernel, out_shape=(jax.ShapeDtypeStruct((STEPS + 1...  212 us
    unnamed x1, local copies, waits for them, and re-layouts  4.5 us

profile of v6, /device:TPU:0, one launch (start us, length us, event | category | flops | bytes accessed | tf_op | source)
XLA Modules:
  0.0 218.5 jit_solution(6079812272950525650)
XLA Ops:
  0.6 211.9 %shard_map.67 = (f32[7,1024,128]{2,1,0:T(8,128)}, f32[6,8,128]{2,1,0:T(8,128)}) custom-call(f32[8192,128]{1,0:T(8,128)} %bitcast.6, bf16[16,256,256]{2,1,0:T(8,128)(2,1)} %left_hbm.1, bf16[16,16,16]{2,1,0:T(8,128)(2,1)} %two_ref.1, bf16[16,128,256]{2,1,0:T(8,128)(2,1)} %right_hbm.1), custom_call_target="tpu_custom_call" | custom-call | tf_op jit(solution)/shard_map/pallas_call | solution.py:530
  212.5 1.5 slice_reduce_fusion
  214.0 4.5 %copy.10 = f32[7,64,4,4,128]{4,3,2,1,0:T(4,128)} copy(f32[7,64,4,4,128]{4,3,2,1,0:T(4,128)} %bitcast.7) | data formatting | bytes 7340032

commit v7 on v6

--- a/solution.py
+++ b/solution.py
@@ -177,22 +177,22 @@
             u_got(h, m, s).wait_recv()
             u_relay(h, m, s).start()
 
-    def r_stage(h, k0, nk, m):
+    def r_stage(h, k0, nk, n):
         lhs = rw[pl.ds(k0, nk)].reshape(nk * COLS, BOND)
-        rhs = jnp.concatenate([uT[h, 4 * m + i] for i in range(4)], axis=1)
+        rhs = jnp.concatenate([uT[h, 2 * n], uT[h, 2 * n + 1]], axis=1)
         res = jnp.dot(lhs, rhs, preferred_element_type=F32).astype(BF16)
-        for i in range(4):
-            yb[pl.ds(k0, nk), 4 * m + i] = res[:, HALF * i:HALF * (i + 1)].reshape(nk, COLS, HALF)
-
-    def wl_stage(h, k0, nk, buf=0):
+        yb[pl.ds(k0, nk), 2 * n] = res[:, :HALF].reshape(nk, COLS, HALF)
+        yb[pl.ds(k0, nk), 2 * n + 1] = res[:, HALF:].reshape(nk, COLS, HALF)
+
+    def wl_stage(h, k0, nk):
         for k in range(nk):
             rhs = jnp.concatenate(
                 [yb[k0 + k, :, pl.ds(16 * i, 16), :].reshape(BOND, HALF) for i in range(2)], axis=1)
             res = jnp.dot(bd[k0 + k], rhs, preferred_element_type=F32).astype(BF16)
             for i in range(2):
-                zb[buf, :, pl.ds(16 * i, 16), pl.ds(HALF * k, HALF)] = (
+                zb[:, pl.ds(16 * i, 16), pl.ds(HALF * k, HALF)] = (
                     res[:, HALF * i:HALF * (i + 1)].reshape(PAIR, 16, HALF))
-        lhs = zb[buf, :, :, pl.ds(0, nk * HALF)].reshape(PAIR * COLS, nk * HALF)
+        lhs = zb[:, :, pl.ds(0, nk * HALF)].reshape(PAIR * COLS, nk * HALF)
         rhs = lw[pl.ds(k0, nk), pl.ds(pl.multiple_of(HALF * h, HALF), HALF), :].reshape(nk * HALF, BOND)
         res = jnp.dot(lhs, rhs, preferred_element_type=F32)
         acc[...] = acc[...] + res.reshape(PAIR, COLS, BOND)
@@ -212,8 +212,8 @@
             bd[g * 8 + k] = (full * mask[...]).astype(BF16)
 
     def first_half(h, k0, nk):
-        for m in range(4):
-            r_stage(h, k0, nk, m)
+        for n in range(8):
+            r_stage(h, k0, nk, n)
         wl_stage(h, k0, nk)
 
     def bd_group(g, carry):
@@ -245,30 +245,30 @@
             for i in range(4):
                 l_step(i, 0).wait_recv()
             lax.fori_loop(0, 8, l_unpack, 5)
+            r_send(1).wait_recv()
+            r_send(2).wait_recv()
+
+        def half(h, carry):
+            first_half(h, s * BLOCK, BLOCK)
+            return carry
+
+        lax.fori_loop(0, 2, half, 0)
+        return carry
+
+    def last_group(g, carry):
+        @pl.when(g == 6)
+        def _():
             for i in range(4):
                 l_step(i, 1).wait_recv()
                 l_step(i, 2).start()
-            r_send(1).wait_recv()
-            r_send(2).wait_recv()
-
-        def half(h, carry):
-            first_half(h, s * BLOCK, BLOCK)
-            return carry
-
-        lax.fori_loop(0, 2, half, 0)
-        return carry
-
-    def last_group(g, carry):
-        @pl.when(g == 6)
-        def _():
             lax.fori_loop(0, 8, l_unpack, 6)
+            r_send(3).wait_recv()
+
+        @pl.when(g == 7)
+        def _():
             for i in range(4):
                 l_step(i, 2).wait_recv()
             lax.fori_loop(0, 8, l_unpack, 7)
-            r_send(3).wait_recv()
-
-        @pl.when(g == 7)
-        def _():
             r_send(4).wait_recv()
 
         def half(h, carry):
@@ -289,34 +289,29 @@
 
         return carry
 
-    def u_all(h, m):
+    def later_r(h, m):
         u_got(h, m, 3).wait_recv()
         for s in range(3):
             u_relayed(h, m, s).wait_recv()
-
-    def later_r(h, m):
-        u_all(h, m)
-        r_stage(h, 0, TERMS, m)
+        for n in range(2):
+            r_stage(h, 0, TERMS, 2 * m + n)
 
     def gather_wl(s, carry):
         relay_all(1, s)
         wl_stage(0, s * BLOCK, BLOCK)
         return carry
 
-    def second():
-        for m in range(4):
-            u_all(1, m)
-        for m in range(4):
-            r_stage(1, 0, TERMS, m)
-        for s in range(4):
-            wl_stage(1, s * BLOCK, BLOCK, s % 2)
-
-    def sent(m, carry):
+    def second_r(m, carry):
+        later_r(1, m)
         for h in range(2):
             for s in range(4):
                 u_own(h, m, s).wait_send()
             for s in range(3):
                 u_relay(h, m, s).wait_send()
+        return carry
+
+    def second_wl(s, carry):
+        wl_stage(1, s * BLOCK, BLOCK)
         return carry
 
     def x_copy(par, q):
@@ -390,8 +385,8 @@
             lax.fori_loop(0, 5, gather_r, 0)
             lax.fori_loop(0, 4, gather_wl, 0)
             x_start((j + 1) % 2)
-            second()
-            lax.fori_loop(0, 4, sent, 0)
+            lax.fori_loop(0, 4, second_r, 0)
+            lax.fori_loop(0, 4, second_wl, 0)
 
         cur = j % 3
         prev = (j + 2) % 3
@@ -549,7 +544,7 @@
                 pltpu.VMEM((4, PAIR, BOND), BF16),
                 pltpu.VMEM((BOND, BOND), F32),
                 pltpu.VMEM((TERMS, PAIR, COLS, HALF), BF16),
-                pltpu.VMEM((2, PAIR, COLS, BLOCK * HALF), BF16),
+                pltpu.VMEM((PAIR, COLS, BLOCK * HALF), BF16),
                 pltpu.VMEM((2, PAIR, BOND, HALF), BF16),
                 pltpu.VMEM((PAIR, COLS, BOND), F32),
                 pltpu.VMEM((3, PAIR, COLS, BOND), F32),

time: 219 us -> 215 us (0.982)
  Pallas kernels: 212 us -> 209 us
    pallas_call x1, Pallas kernels: 212 us -> 209 us  [body_fn(): pl.pallas_call(lanczos_kernel, out_shape=(jax.ShapeDtypeStruct((STEPS + 1...]
where the time goes in v7:
time: 215 us
  Pallas kernels  209 us (97%)
  local copies, waits for them, and re-layouts  5.96 us (3%)
    pallas_call x1, Pallas kernels, body_fn(): pl.pallas_call(lanczos_kernel, out_shape=(jax.ShapeDtypeStruct((STEPS + 1...  209 us
    unnamed x1, local copies, waits for them, and re-layouts  4.5 us

profile of v7, /device:TPU:0, one launch (start us, length us, event | category | flops | bytes accessed | tf_op | source)
XLA Modules:
  0.0 215.2 jit_solution(5806797311935714257)
XLA Ops:
  0.6 208.6 %shard_map.67 = (f32[7,1024,128]{2,1,0:T(8,128)}, f32[6,8,128]{2,1,0:T(8,128)}) custom-call(f32[8192,128]{1,0:T(8,128)} %bitcast.6, bf16[16,256,256]{2,1,0:T(8,128)(2,1)} %left_hbm.1, bf16[16,16,16]{2,1,0:T(8,128)(2,1)} %two_ref.1, bf16[16,128,256]{2,1,0:T(8,128)(2,1)} %right_hbm.1), custom_call_target="tpu_custom_call" | custom-call | tf_op jit(solution)/shard_map/pallas_call | solution.py:525
  209.2 1.5 slice_reduce_fusion
  210.7 4.5 %copy.10 = f32[7,64,4,4,128]{4,3,2,1,0:T(4,128)} copy(f32[7,64,4,4,128]{4,3,2,1,0:T(4,128)} %bitcast.7) | data formatting | bytes 7340032

commit v8 on v4

--- a/solution.py
+++ b/solution.py
@@ -184,16 +184,16 @@
         yb[pl.ds(k0, nk), 2 * n] = res[:, :HALF].reshape(nk, COLS, HALF)
         yb[pl.ds(k0, nk), 2 * n + 1] = res[:, HALF:].reshape(nk, COLS, HALF)
 
-    def wl_stage(h, s):
+    def wl_stage(h, s, buf=0):
         k0 = s * BLOCK
         for k in range(BLOCK):
             rhs = jnp.concatenate(
                 [yb[k0 + k, :, pl.ds(16 * i, 16), :].reshape(BOND, HALF) for i in range(2)], axis=1)
             res = jnp.dot(bd[k0 + k], rhs, preferred_element_type=F32).astype(BF16)
             for i in range(2):
-                zb[:, pl.ds(16 * i, 16), pl.ds(HALF * k, HALF)] = (
+                zb[buf, :, pl.ds(16 * i, 16), pl.ds(HALF * k, HALF)] = (
                     res[:, HALF * i:HALF * (i + 1)].reshape(PAIR, 16, HALF))
-        lhs = zb[...].reshape(PAIR * COLS, BLOCK * HALF)
+        lhs = zb[buf].reshape(PAIR * COLS, BLOCK * HALF)
         rhs = lw[pl.ds(k0, BLOCK), pl.ds(pl.multiple_of(HALF * h, HALF), HALF), :].reshape(BLOCK * HALF, BOND)
         res = jnp.dot(lhs, rhs, preferred_element_type=F32)
         acc[...] = acc[...] + res.reshape(PAIR, COLS, BOND)
@@ -304,10 +304,6 @@
                 u_relay(h, m, s).wait_send()
         return carry
 
-    def second_wl(s, carry):
-        wl_stage(1, s)
-        return carry
-
     def x_copy(par, q):
         dest = (t + q) % 4
         return rdma(xs.at[dest], xr.at[par, t], x_ssem.at[q - 1], x_rsem.at[par, q - 1], (y, dest))
@@ -379,7 +375,8 @@
             lax.fori_loop(0, 4, gather_wl, 0)
             x_start((j + 1) % 2)
             lax.fori_loop(0, 4, second_r, 0)
-            lax.fori_loop(0, 4, second_wl, 0)
+            for s in range(4):
+                wl_stage(1, s, s % 2)
 
         cur = j % 3
         prev = (j + 2) % 3
@@ -460,7 +457,7 @@
                 uT[0, p, rows, :] = v[:, :HALF].astype(BF16)
                 uT[1, p, rows, :] = v[:, HALF:].astype(BF16)
 
-            for s in range(4):
+            for s in (2, 0, 1, 3):
                 u_own(0, m, s).start()
             return carry
 
@@ -468,7 +465,7 @@
         def _():
             lax.fori_loop(0, 4, pass3, 0)
             for m in range(4):
-                for s in range(4):
+                for s in (2, 0, 1, 3):
                     u_own(1, m, s).start()
 
         @pl.when((j > 0) & (j < STEPS - 1))
@@ -537,7 +534,7 @@
                 pltpu.VMEM((4, PAIR, BOND), BF16),
                 pltpu.VMEM((BOND, BOND), F32),
                 pltpu.VMEM((TERMS, PAIR, COLS, HALF), BF16),
-                pltpu.VMEM((PAIR, COLS, BLOCK * HALF), BF16),
+                pltpu.VMEM((2, PAIR, COLS, BLOCK * HALF), BF16),
                 pltpu.VMEM((2, PAIR, BOND, HALF), BF16),
                 pltpu.VMEM((PAIR, COLS, BOND), F32),
                 pltpu.VMEM((3, PAIR, COLS, BOND), F32),

time: 212 us -> 210 us (level)
  no operation moved by 1% of the time
where the time goes in v8:
time: 210 us
  Pallas kernels  203 us (97%)
  local copies, waits for them, and re-layouts  5.96 us (3%)
    pallas_call x1, Pallas kernels, body_fn(): pl.pallas_call(lanczos_kernel, out_shape=(jax.ShapeDtypeStruct((STEPS + 1...  203 us
    unnamed x1, local copies, waits for them, and re-layouts  4.5 us

profile of v8, /device:TPU:0, one launch (start us, length us, event | category | flops | bytes accessed | tf_op | source)
XLA Modules:
  0.0 209.7 jit_solution(9549000144647100546)
XLA Ops:
  0.6 203.1 %shard_map.67 = (f32[7,1024,128]{2,1,0:T(8,128)}, f32[6,8,128]{2,1,0:T(8,128)}) custom-call(f32[8192,128]{1,0:T(8,128)} %bitcast.6, bf16[16,256,256]{2,1,0:T(8,128)(2,1)} %left_hbm.1, bf16[16,16,16]{2,1,0:T(8,128)(2,1)} %two_ref.1, bf16[16,128,256]{2,1,0:T(8,128)(2,1)} %right_hbm.1), custom_call_target="tpu_custom_call" | custom-call | tf_op jit(solution)/shard_map/pallas_call | solution.py:515
  203.8 1.5 slice_reduce_fusion
  205.2 4.5 %copy.10 = f32[7,64,4,4,128]{4,3,2,1,0:T(4,128)} copy(f32[7,64,4,4,128]{4,3,2,1,0:T(4,128)} %bitcast.7) | data formatting | bytes 7340032

commit v9 on v8

--- a/solution.py
+++ b/solution.py
@@ -18,7 +18,7 @@
 
 
 def lanczos_kernel(
-    wf_hbm, left_hbm, two_ref, right_hbm, kry_hbm, ab_ref,
+    wf_hbm, left_hbm, two_ref, right_hbm, kry_hbm, ab_ref, one_ref,
     wfv, rw, lw, lx, bd, wt, mask, yb, zb, uT, acc, vb, tmp, st, betas, coef, xs, xr, osb,
     loc_sem, w_ssem, w_rsem, r_ssem, r_rsem, l_ssem, l_rsem, lx_ssem, lx_rsem,
     u_ssem, u_rsem, f_ssem, f_rsem, st_ssem, st_rsem, x_ssem, x_rsem, o_sem,
@@ -147,6 +147,7 @@
         osb[0, pl.ds(p, 64, stride=16), :] = jnp.where(y == 0, lo, hi) / scale
     vb[2] = jnp.zeros((PAIR, COLS, BOND), F32)
     betas[...] = jnp.zeros((1, 128), F32)
+    one_ref[...] = jnp.ones((1, 128), F32)
 
     def out_copy(j):
         return pltpu.make_async_copy(osb.at[j % 2], kry_hbm.at[j], o_sem.at[j % 2])
@@ -154,23 +155,24 @@
     out_copy(0).start()
 
     def u_part(h, m, dev):
-        return uT.at[h, pl.ds(4 * m, 4), pl.ds(pl.multiple_of(32 * dev, 32), 32), :]
+        n = 2 + 2 * h
+        return uT.at[h, pl.ds(n * m, n), pl.ds(pl.multiple_of(32 * dev, 32), 32), :]
 
     def u_own(h, m, s):
         part = u_part(h, m, me)
-        return rdma(part, part, u_ssem.at[h, m, s], u_rsem.at[h, m, s], (xnb, ynb, diag, sib)[s])
+        return rdma(part, part, u_ssem.at[8 * h + m, s], u_rsem.at[8 * h + m, s], (xnb, ynb, diag, sib)[s])
 
     def u_got(h, m, s):
         part = u_part(h, m, (near + (me + flip,))[s])
-        return rdma(part, part, u_ssem.at[h, m, s], u_rsem.at[h, m, s], (xnb, ynb, diag, sib)[s])
+        return rdma(part, part, u_ssem.at[8 * h + m, s], u_rsem.at[8 * h + m, s], (xnb, ynb, diag, sib)[s])
 
     def u_relay(h, m, s):
         part = u_part(h, m, near[s])
-        return rdma(part, part, f_ssem.at[h, m, s], f_rsem.at[h, m, s], sib)
+        return rdma(part, part, f_ssem.at[8 * h + m, s], f_rsem.at[8 * h + m, s], sib)
 
     def u_relayed(h, m, s):
         part = u_part(h, m, near[s] + flip)
-        return rdma(part, part, f_ssem.at[h, m, s], f_rsem.at[h, m, s], sib)
+        return rdma(part, part, f_ssem.at[8 * h + m, s], f_rsem.at[8 * h + m, s], sib)
 
     def relay_all(h, m):
         for s in range(3):
@@ -273,7 +275,7 @@
         return carry
 
     def gather_r(i, carry):
-        @pl.when(i < 4)
+        @pl.when(i < 8)
         def _():
             relay_all(0, i)
 
@@ -287,8 +289,8 @@
         u_got(h, m, 3).wait_recv()
         for s in range(3):
             u_relayed(h, m, s).wait_recv()
-        for n in range(2):
-            r_stage(h, 0, TERMS, 2 * m + n)
+        for n in range(1 + h):
+            r_stage(h, 0, TERMS, (1 + h) * m + n)
 
     def gather_wl(s, carry):
         relay_all(1, s)
@@ -297,11 +299,11 @@
 
     def second_r(m, carry):
         later_r(1, m)
-        for h in range(2):
+        for h, k in ((0, 2 * m), (0, 2 * m + 1), (1, m)):
             for s in range(4):
-                u_own(h, m, s).wait_send()
+                u_own(h, k, s).wait_send()
             for s in range(3):
-                u_relay(h, m, s).wait_send()
+                u_relay(h, k, s).wait_send()
         return carry
 
     def x_copy(par, q):
@@ -371,7 +373,7 @@
 
         @pl.when(j > 0)
         def _():
-            lax.fori_loop(0, 5, gather_r, 0)
+            lax.fori_loop(0, 9, gather_r, 0)
             lax.fori_loop(0, 4, gather_wl, 0)
             x_start((j + 1) % 2)
             lax.fori_loop(0, 4, second_r, 0)
@@ -457,8 +459,9 @@
                 uT[0, p, rows, :] = v[:, :HALF].astype(BF16)
                 uT[1, p, rows, :] = v[:, HALF:].astype(BF16)
 
-            for s in (2, 0, 1, 3):
-                u_own(0, m, s).start()
+            for i in range(2):
+                for s in (2, 0, 1, 3):
+                    u_own(0, 2 * m + i, s).start()
             return carry
 
         @pl.when(j < STEPS - 1)
@@ -512,11 +515,12 @@
         bond, phys = wavefunc.shape[0], wavefunc.shape[1]
         wf = wavefunc.reshape(bond, phys, phys, 2, 128).transpose(0, 1, 3, 2, 4).reshape(-1, 128)
         dma = pltpu.SemaphoreType.DMA
-        kry, ab = pl.pallas_call(
+        kry, ab, one = pl.pallas_call(
             lanczos_kernel,
             out_shape=(
                 jax.ShapeDtypeStruct((STEPS + 1, 64 * PAIR, 128), F32),
                 jax.ShapeDtypeStruct((STEPS, 8, 128), F32),
+                jax.ShapeDtypeStruct((1, 128), F32),
             ),
             in_specs=[
                 pl.BlockSpec(memory_space=pl.ANY),
@@ -524,7 +528,8 @@
                 pl.BlockSpec(memory_space=pltpu.VMEM),
                 pl.BlockSpec(memory_space=pl.ANY),
             ],
-            out_specs=(pl.BlockSpec(memory_space=pl.ANY), pl.BlockSpec(memory_space=pltpu.VMEM)),
+            out_specs=(pl.BlockSpec(memory_space=pl.ANY), pl.BlockSpec(memory_space=pltpu.VMEM),
+                       pl.BlockSpec(memory_space=pltpu.VMEM)),
             scratch_shapes=[
                 pltpu.VMEM((8192, 128), F32),
                 pltpu.VMEM((TERMS, COLS, BOND), BF16),
@@ -550,8 +555,8 @@
                 dma((5,)), dma((5,)),
                 dma((9,)), dma((9,)),
                 dma((3, 4)), dma((3, 4)),
-                dma((2, 4, 4)), dma((2, 4, 4)),
-                dma((2, 4, 3)), dma((2, 4, 3)),
+                dma((12, 4)), dma((12, 4)),
+                dma((12, 3)), dma((12, 3)),
                 dma((7,)), dma((7,)),
                 dma((3,)), dma((2, 3)),
                 dma((2,)),
@@ -559,6 +564,7 @@
             compiler_params=pltpu.CompilerParams(
                 collective_id=0, has_side_effects=True, vmem_limit_bytes=66 * 1000 * 1000),
         )(wf, left_loc, two_loc, right_loc)
+        kry = kry * one
         krylov = kry.reshape(STEPS + 1, 64, phys, phys, 128)
         return krylov, ab[:, 0, 0], ab[:, 1, 0]
 

time: 210 us -> 210 us (level)
  local copies, waits for them, and re-layouts: 5.96 us -> 1.45 us
  other arithmetic: 0 us -> 4.12 us
    unnamed x1 -> x0, local copies, waits for them, and re-layouts: 4.5 us -> none
    mul x0 -> x1, other arithmetic: none -> 4.12 us  [body_fn(): kry = kry * one]
where the time goes in v9:
time: 210 us
  Pallas kernels  204 us (97%)
  other arithmetic  4.12 us (2%)
    pallas_call x1, Pallas kernels, body_fn(): pl.pallas_call(lanczos_kernel, out_shape=(jax.ShapeDtypeStruct((STEPS + 1...  204 us

profile of v9, /device:TPU:0, one launch (start us, length us, event | category | flops | bytes accessed | tf_op | source)
XLA Modules:
  0.0 209.9 jit_solution(8890314210477041826)
XLA Ops:
  0.6 203.7 %shard_map.67 = (f32[7,1024,128]{2,1,0:T(8,128)}, f32[6,8,128]{2,1,0:T(8,128)}, f32[1,128]{1,0:T(1,128)}) custom-call(f32[8192,128]{1,0:T(8,128)} %bitcast.7, bf16[16,256,256]{2,1,0:T(8,128)(2,1)} %left_hbm.1, bf16[16,16,16]{2,1,0:T(8,128)(2,1)} %two_ref.1, bf16[16,128,256]{2,1,0:T(8,128)(2,1)} %right_hbm.1), custom_call_target="tpu_custom_call" | custom-call | tf_op jit(solution)/shard_map/pallas_call | solution.py:518
  204.3 4.1 %broadcast_multiply_fusion = f32[7,1024,128]{2,1,0:T(8,128)} fusion(f32[7,1024,128]{2,1,0:T(8,128)} %get-tuple-element.6, f32[128]{0:T(128)} %bitcast.9), kind=kLoop, calls=%fused_computation | loop fusion | flops 917504 | bytes 7340544 | tf_op jit(solution)/shard_map/mul | solution.py:567
  208.4 1.5 slice_reduce_fusion

commit v10 on v8

--- a/solution.py
+++ b/solution.py
@@ -18,7 +18,7 @@
 
 
 def lanczos_kernel(
-    wf_hbm, left_hbm, two_ref, right_hbm, kry_hbm, ab_ref,
+    wf_hbm, left_hbm, two_ref, right_hbm, kry_hbm, ab_ref, one_ref,
     wfv, rw, lw, lx, bd, wt, mask, yb, zb, uT, acc, vb, tmp, st, betas, coef, xs, xr, osb,
     loc_sem, w_ssem, w_rsem, r_ssem, r_rsem, l_ssem, l_rsem, lx_ssem, lx_rsem,
     u_ssem, u_rsem, f_ssem, f_rsem, st_ssem, st_rsem, x_ssem, x_rsem, o_sem,
@@ -147,6 +147,7 @@
         osb[0, pl.ds(p, 64, stride=16), :] = jnp.where(y == 0, lo, hi) / scale
     vb[2] = jnp.zeros((PAIR, COLS, BOND), F32)
     betas[...] = jnp.zeros((1, 128), F32)
+    one_ref[...] = jnp.ones((1, 128), F32)
 
     def out_copy(j):
         return pltpu.make_async_copy(osb.at[j % 2], kry_hbm.at[j], o_sem.at[j % 2])
@@ -233,18 +234,25 @@
             w_send(1).wait_recv()
             w_send(2).wait_recv()
 
+        for i in range(1, 3):
+            @pl.when(s == i)
+            def _(i=i):
+                l_take(i)
+
+        @pl.when(s == 3)
+        def _():
+            for i in range(4):
+                l_step(i, 1).wait_recv()
+                l_step(i, 2).start()
+
         lax.fori_loop(0, 2, bd_group, s)
 
-        @pl.when(s < 2)
-        def _():
-            for i in range(2):
-                @pl.when(s == i)
-                def _(i=i):
-                    l_take(i)
+        @pl.when(s == 0)
+        def _():
+            l_take(0)
 
         @pl.when(s == 2)
         def _():
-            l_take(2)
             l_take(3)
             for i in range(4):
                 l_step(i, 0).wait_recv()
@@ -254,9 +262,6 @@
 
         @pl.when(s == 3)
         def _():
-            for i in range(4):
-                l_step(i, 1).wait_recv()
-                l_step(i, 2).start()
             for i in range(4):
                 l_step(i, 2).wait_recv()
             lax.fori_loop(0, 16, l_unpack, s)
@@ -512,11 +517,12 @@
         bond, phys = wavefunc.shape[0], wavefunc.shape[1]
         wf = wavefunc.reshape(bond, phys, phys, 2, 128).transpose(0, 1, 3, 2, 4).reshape(-1, 128)
         dma = pltpu.SemaphoreType.DMA
-        kry, ab = pl.pallas_call(
+        kry, ab, one = pl.pallas_call(
             lanczos_kernel,
             out_shape=(
                 jax.ShapeDtypeStruct((STEPS + 1, 64 * PAIR, 128), F32),
                 jax.ShapeDtypeStruct((STEPS, 8, 128), F32),
+                jax.ShapeDtypeStruct((1, 128), F32),
             ),
             in_specs=[
                 pl.BlockSpec(memory_space=pl.ANY),
@@ -524,7 +530,8 @@
                 pl.BlockSpec(memory_space=pltpu.VMEM),
                 pl.BlockSpec(memory_space=pl.ANY),
             ],
-            out_specs=(pl.BlockSpec(memory_space=pl.ANY), pl.BlockSpec(memory_space=pltpu.VMEM)),
+            out_specs=(pl.BlockSpec(memory_space=pl.ANY), pl.BlockSpec(memory_space=pltpu.VMEM),
+                       pl.BlockSpec(memory_space=pltpu.VMEM)),
             scratch_shapes=[
                 pltpu.VMEM((8192, 128), F32),
                 pltpu.VMEM((TERMS, COLS, BOND), BF16),
@@ -559,6 +566,7 @@
             compiler_params=pltpu.CompilerParams(
                 collective_id=0, has_side_effects=True, vmem_limit_bytes=66 * 1000 * 1000),
         )(wf, left_loc, two_loc, right_loc)
+        kry = kry * one
         krylov = kry.reshape(STEPS + 1, 64, phys, phys, 128)
         return krylov, ab[:, 0, 0], ab[:, 1, 0]
 

time: 210 us -> 208 us (level)
  local copies, waits for them, and re-layouts: 5.96 us -> 1.45 us
  other arithmetic: 0 us -> 4.12 us
    unnamed x1 -> x0, local copies, waits for them, and re-layouts: 4.5 us -> none
    mul x0 -> x1, other arithmetic: none -> 4.12 us  [body_fn(): kry = kry * one]
where the time goes in v10:
time: 208 us
  Pallas kernels  202 us (97%)
  other arithmetic  4.12 us (2%)
    pallas_call x1, Pallas kernels, body_fn(): pl.pallas_call(lanczos_kernel, out_shape=(jax.ShapeDtypeStruct((STEPS + 1...  202 us

profile of v10, /device:TPU:0, one launch (start us, length us, event | category | flops | bytes accessed | tf_op | source)
XLA Modules:
  0.0 207.8 jit_solution(11678865054682302317)
XLA Ops:
  0.6 201.6 %shard_map.67 = (f32[7,1024,128]{2,1,0:T(8,128)}, f32[6,8,128]{2,1,0:T(8,128)}, f32[1,128]{1,0:T(1,128)}) custom-call(f32[8192,128]{1,0:T(8,128)} %bitcast.7, bf16[16,256,256]{2,1,0:T(8,128)(2,1)} %left_hbm.1, bf16[16,16,16]{2,1,0:T(8,128)(2,1)} %two_ref.1, bf16[16,128,256]{2,1,0:T(8,128)(2,1)} %right_hbm.1), custom_call_target="tpu_custom_call" | custom-call | tf_op jit(solution)/shard_map/pallas_call | solution.py:520
  202.2 4.1 %broadcast_multiply_fusion = f32[7,1024,128]{2,1,0:T(8,128)} fusion(f32[7,1024,128]{2,1,0:T(8,128)} %get-tuple-element.6, f32[128]{0:T(128)} %bitcast.9), kind=kLoop, calls=%fused_computation | loop fusion | flops 917504 | bytes 7340544 | tf_op jit(solution)/shard_map/mul | solution.py:569
  206.4 1.5 slice_reduce_fusion
